TPU v7x, 128 devices: a whole 4x4x4 slice. The times are simulated.
128 devices in a mesh: px: 16 (over y, z), py: 8 (over x, core).
Axes of the slice: x: 4, y: 4, z: 4, core: 2. Of those that a mesh axis runs over, the one named last changes fastest.
Arguments:
- initial_field: float32 [1, 2048, 2048], P(None, ('px', 'py')), may hold values from -6 to 6
- target_field: float32 [1, 2048, 2048], P(None, ('px', 'py')), may hold values from -6 to 6
- forcing: float32 [2, 2048, 2048], P(None, ('px', 'py')), may hold values from -6 to 6
Outputs:
- next_field: float32 [1, 2048, 2048], P(None, ('px', 'py'))
- objective: float32 [], replicated
- field_grad: float32 [1, 2048, 2048], P(None, ('px', 'py'))
- forcing_grad: float32 [2, 2048, 2048], P(None, ('px', 'py'))
All inputs are finite; a program needn't handle non-finite values.
Results may differ from a plain program's by a relative error of at most 0.00014.
Values sent between devices are 32-bit elements; how exact they have to be, the bound alone decides.
A program may use at most 64 MiB of HBM per device.

v0:
```python
import math

import jax
import jax.numpy as jnp
from jax import lax
from jax.sharding import Mesh
from jax.sharding import PartitionSpec as P

PX_PY = ("px_0", "px_1", "py_0", "py_1")
PX = ("px_0", "px_1")
PY = ("py_0", "py_1")


time_step = 0.25
highest = lax.Precision.HIGHEST


def in_blocks(shard, dim, length):
    dims = shard.shape
    tiles = shard.reshape(*dims[:dim], length, dims[dim] // length, *dims[dim + 1 :])
    return jnp.moveaxis(tiles, dim, 0)


def laid_out(tiles, dim):
    tiles = jnp.moveaxis(tiles, 0, dim)
    dims = tiles.shape
    return tiles.reshape(*dims[:dim], dims[dim] * dims[dim + 1], *dims[dim + 2 :])


def one_exchange(shard, axis, axes, splits, concats):
    sizes = [lax.axis_size(a) for a in axes]
    tiles = in_blocks(shard, splits[0], sizes[0])
    tiles = jnp.moveaxis(in_blocks(tiles, splits[1] + 1, sizes[1]), 0, 1)
    inside = tiles.shape[2:]
    tiles = tiles.reshape(-1, *inside)
    tiles = lax.all_to_all(tiles, axis, split_axis=0, concat_axis=0, tiled=True)
    tiles = laid_out(tiles.reshape(*sizes, *inside), concats[0] + 1)
    return laid_out(tiles, concats[1])


def one_axis_at_a_time(shard, axes):
    for axis in axes:
        shard = lax.psum(shard, axis)
    return shard


def factor_pair(length):
    first_len = int(math.isqrt(length))
    while length % first_len:
        first_len -= 1
    return (first_len, length // first_len)


def phases(row_count, col_count, period, sign_value, factor):
    product = (
        jnp.arange(row_count, dtype=jnp.int32)[:, None]
        * jnp.arange(col_count, dtype=jnp.int32)[None, :]
        % period
    )
    angles = product.astype(jnp.float32) * (2.0 * math.pi / period)
    return (factor * jnp.cos(angles), sign_value * factor * jnp.sin(angles))


def complex_einsum(formula, left_real, left_imag, table_pair):
    real_term = jnp.einsum(formula, left_real, table_pair[0], precision=highest)
    imag_term = jnp.einsum(formula, left_real, table_pair[1], precision=highest)
    if left_imag is None:
        return (real_term, imag_term)
    real_term = real_term - jnp.einsum(formula, left_imag, table_pair[1], precision=highest)
    imag_term = imag_term + jnp.einsum(formula, left_imag, table_pair[0], precision=highest)
    return (real_term, imag_term)


def transform(real_part, imag_part, sign_value, leading, real_only):
    if leading:
        members, length, span_rows = real_part.shape
        first_len, second_len = factor_pair(length)
        new_shape = (members, first_len, second_len, span_rows)
        formula = "mabr,ak->mrkb"
    else:
        members, span_rows, length = real_part.shape
        first_len, second_len = factor_pair(length)
        new_shape = (members, span_rows, first_len, second_len)
        formula = "mrab,ak->mrkb"
    shaped_real = real_part.reshape(new_shape)
    shaped_imag = None if imag_part is None else imag_part.reshape(new_shape)
    sectioned_out = complex_einsum(
        formula, shaped_real, shaped_imag, phases(first_len, first_len, first_len, sign_value, 1.0)
    )
    twiddle = phases(first_len, second_len, length, sign_value, 1.0 / math.sqrt(length))
    turned_real = sectioned_out[0] * twiddle[0] - sectioned_out[1] * twiddle[1]
    turned_imag = sectioned_out[0] * twiddle[1] + sectioned_out[1] * twiddle[0]
    last_table = phases(second_len, second_len, second_len, sign_value, 1.0)
    final_formula = "mrkb,bq->mrqk"
    if real_only:
        out_real = jnp.einsum(final_formula, turned_real, last_table[0], precision=highest)
        out_real = out_real - jnp.einsum(
            final_formula, turned_imag, last_table[1], precision=highest
        )
        return (out_real.reshape(members, span_rows, length), None)
    out_real, out_imag = complex_einsum(final_formula, turned_real, turned_imag, last_table)
    return (
        out_real.reshape(members, span_rows, length),
        out_imag.reshape(members, span_rows, length),
    )


def reorder(block, outer_count, inner_count):
    members, full_len, span_cols = block.shape
    blocks = block.reshape(
        members, inner_count, outer_count, full_len // (outer_count * inner_count), span_cols
    )
    return jnp.swapaxes(blocks, 1, 2).reshape(members, full_len, span_cols)


def regroup(real_part, imag_part):
    moved_real, moved_imag = (
        one_exchange(real_part, PX_PY, (PX, PY), (2, 2), (1, 1)),
        one_exchange(imag_part, PX_PY, (PX, PY), (2, 2), (1, 1)),
    )
    outer_count = lax.axis_size(PX)
    inner_count = lax.axis_size(PY)
    moved_real = reorder(moved_real, outer_count, inner_count)
    moved_imag = reorder(moved_imag, outer_count, inner_count)
    return (moved_real, moved_imag)


def spectral(real_part, imag_part):
    first_pass = transform(real_part, imag_part, -1.0, False, False)
    moved = regroup(first_pass[0], first_pass[1])
    return transform(moved[0], moved[1], -1.0, True, False)


def physical(real_part, imag_part, real_only):
    first_pass = transform(real_part, imag_part, 1.0, False, False)
    moved = regroup(first_pass[0], first_pass[1])
    return transform(moved[0], moved[1], 1.0, True, real_only)


def waves_of(position, count):
    signed = jnp.where(position < count // 2, position, position - count)
    waves = 4.0 * signed.astype(jnp.float32) / count
    derive = jnp.where(position == count // 2, jnp.float32(0.0), waves)
    return (waves, derive)


def per_device(initial_field, target_field, forcing):
    members = initial_field.shape[0]
    full_second = initial_field.shape[2]
    spec_rows = forcing.shape[1]
    full_first = forcing.shape[2]
    device = lax.axis_index(PX_PY)
    position_first = jnp.arange(full_first, dtype=jnp.int32)
    position_second = device * spec_rows + jnp.arange(spec_rows, dtype=jnp.int32)
    wave_first, deriv_first = waves_of(position_first, full_first)
    wave_second, deriv_second = waves_of(position_second, full_second)
    wave_first = wave_first[None, :]
    deriv_first = deriv_first[None, :]
    wave_second = wave_second[:, None]
    deriv_second = deriv_second[:, None]
    wave_square = wave_first * wave_first + wave_second * wave_second
    denominator = 1.0 + time_step * (wave_square * wave_square - wave_square)
    state_real, state_imag = spectral(initial_field, None)
    slope_real = -deriv_first * state_imag - deriv_second * state_real
    slope_imag = deriv_first * state_real - deriv_second * state_imag
    grad_first, grad_second = physical(slope_real, slope_imag, False)
    nonlinear = -0.5 * (grad_first * grad_first + grad_second * grad_second)
    nonlinear_real, nonlinear_imag = spectral(nonlinear, None)
    next_real = (state_real + time_step * (nonlinear_real + forcing[0])) / denominator
    next_imag = (state_imag + time_step * (nonlinear_imag + forcing[1])) / denominator
    next_field, unused_part = physical(next_real, next_imag, True)
    residual = next_field - target_field
    total = one_axis_at_a_time(0.5 * jnp.sum(residual * residual), PX_PY)
    objective = total / (members * full_first * full_second)
    misfit_real, misfit_imag = spectral(residual, None)
    coef_real = misfit_real / denominator
    coef_imag = misfit_imag / denominator
    forcing_grad = time_step * jnp.stack([jnp.sum(coef_real, axis=0), jnp.sum(coef_imag, axis=0)])
    multiplier, unused_other = physical(time_step * coef_real, time_step * coef_imag, True)
    joint_real, joint_imag = spectral(multiplier * grad_first, multiplier * grad_second)
    total_real = coef_real - deriv_first * joint_imag + deriv_second * joint_real
    total_imag = coef_imag + deriv_first * joint_real + deriv_second * joint_imag
    field_grad, unused_last = physical(total_real, total_imag, True)
    return (next_field, objective, field_grad, forcing_grad)


def solution(mesh):
    finer = Mesh(mesh.devices.reshape(4, 4, 4, 2), ("px_0", "px_1", "py_0", "py_1"))
    in_specs = (P(None, PX_PY, None), P(None, PX_PY, None), P(None, PX_PY, None))
    out_specs = (P(None, PX_PY, None), P(), P(None, PX_PY, None), P(None, PX_PY, None))
    return jax.shard_map(
        per_device, mesh=finer, in_specs=in_specs, out_specs=out_specs, check_vma=False
    )
```

profile of v0, /device:TPU:1, one launch (start us, length us, event | category | flops | bytes accessed | tf_op | source)
XLA Modules:
  0.0 366.5 jit_solution(11714185379476792326)
XLA Ops:
  5.6 11.5 %all-to-all-start = ((f32[128,1,256]{2,1,0:T(1,128)}), f32[128,1,256]{2,1,0:T(1,128)S(1)}, u32[]{:S(2)}, u32[]{:S(2)}) async-start(f32[128,1,256]{2,1,0:T(1,128)} %reshape.1397), calls=%async_computation | async-start | bytes 262144 | tf_op jit(solution)/shard_map/all_to_all | solution.py:36
  20.3 6.8 %all-to-all-done = f32[128,1,256]{2,1,0:T(1,128)S(1)} async-done(((f32[128,1,256]{2,1,0:T(1,128)}), f32[128,1,256]{2,1,0:T(1,128)S(1)}, u32[]{:S(2)}, u32[]{:S(2)}) %all-to-all-start) | async-done | bytes 131104 | tf_op jit(solution)/shard_map/all_to_all | solution.py:36
  35.6 5.9 %all-to-all-done.1 = f32[128,1,256]{2,1,0:T(1,128)S(1)} async-done(((f32[128,1,256]{2,1,0:T(1,128)}), f32[128,1,256]{2,1,0:T(1,128)S(1)}, u32[]{:S(2)}, u32[]{:S(2)}) %all-to-all-start.1) | async-done | bytes 131104 | tf_op jit(solution)/shard_map/all_to_all | solution.py:36
  61.6 7.5 %all-to-all-done.2 = f32[128,1,256]{2,1,0:T(1,128)S(1)} async-done(((f32[128,1,256]{2,1,0:T(1,128)}), f32[128,1,256]{2,1,0:T(1,128)S(1)}, u32[]{:S(2)}, u32[]{:S(2)}) %all-to-all-start.2) | async-done | bytes 131104 | tf_op jit(solution)/shard_map/all_to_all | solution.py:36
  69.1 4.8 %all-to-all-start.3 = ((f32[128,1,256]{2,1,0:T(1,128)}), f32[128,1,256]{2,1,0:T(1,128)S(1)}, u32[]{:S(2)}, u32[]{:S(2)}) async-start(f32[128,1,256]{2,1,0:T(1,128)} %reshape.1403), calls=%async_computation.3 | async-start | bytes 262144 | tf_op jit(solution)/shard_map/all_to_all | solution.py:36
  77.3 6.5 %all-to-all-done.3 = f32[128,1,256]{2,1,0:T(1,128)S(1)} async-done(((f32[128,1,256]{2,1,0:T(1,128)}), f32[128,1,256]{2,1,0:T(1,128)S(1)}, u32[]{:S(2)}, u32[]{:S(2)}) %all-to-all-start.3) | async-done | bytes 131104 | tf_op jit(solution)/shard_map/all_to_all | solution.py:36
  100.8 7.5 %all-to-all-done.4 = f32[128,1,256]{2,1,0:T(1,128)S(1)} async-done(((f32[128,1,256]{2,1,0:T(1,128)}), f32[128,1,256]{2,1,0:T(1,128)S(1)}, u32[]{:S(2)}, u32[]{:S(2)}) %all-to-all-start.4) | async-done | bytes 131104 | tf_op jit(solution)/shard_map/all_to_all | solution.py:36
  116.2 6.5 %all-to-all-done.5 = f32[128,1,256]{2,1,0:T(1,128)S(1)} async-done(((f32[128,1,256]{2,1,0:T(1,128)}), f32[128,1,256]{2,1,0:T(1,128)S(1)}, u32[]{:S(2)}, u32[]{:S(2)}) %all-to-all-start.5) | async-done | bytes 131104 | tf_op jit(solution)/shard_map/all_to_all | solution.py:36
  135.5 4.8 %all-to-all-start.6 = ((f32[128,1,256]{2,1,0:T(1,128)}), f32[128,1,256]{2,1,0:T(1,128)S(1)}, u32[]{:S(2)}, u32[]{:S(2)}) async-start(f32[128,1,256]{2,1,0:T(1,128)} %reshape.1409), calls=%async_computation.6 | async-start | bytes 262144 | tf_op jit(solution)/shard_map/all_to_all | solution.py:36
  142.8 7.4 %all-to-all-done.6 = f32[128,1,256]{2,1,0:T(1,128)S(1)} async-done(((f32[128,1,256]{2,1,0:T(1,128)}), f32[128,1,256]{2,1,0:T(1,128)S(1)}, u32[]{:S(2)}, u32[]{:S(2)}) %all-to-all-start.6) | async-done | bytes 131104 | tf_op jit(solution)/shard_map/all_to_all | solution.py:36
  157.9 6.6 %all-to-all-done.7 = f32[128,1,256]{2,1,0:T(1,128)S(1)} async-done(((f32[128,1,256]{2,1,0:T(1,128)}), f32[128,1,256]{2,1,0:T(1,128)S(1)}, u32[]{:S(2)}, u32[]{:S(2)}) %all-to-all-start.7) | async-done | bytes 131104 | tf_op jit(solution)/shard_map/all_to_all | solution.py:36
  171.4 7.3 %psum.28 = f32[]{:T(128)} all-reduce(f32[]{:T(128)S(6)} %mul_shard_map.3), channel_id=1, replica_groups=mesh['px_0'=4,'px_1'=4,'py_0'=4,'py_1'=2] {'px_0'}, use_global_device_ids=true, to_apply=%region_1.2 | all-reduce | flops 1 | bytes 8 | tf_op jit(solution)/shard_map/psum | solution.py:43
  178.7 7.3 %psum.29 = f32[]{:T(128)} all-reduce(f32[]{:T(128)} %psum.28), channel_id=1, replica_groups=mesh['px_0'=4,'px_1'=4,'py_0'=4,'py_1'=2] {'px_1'}, use_global_device_ids=true, to_apply=%region_2.3 | all-reduce | flops 1 | bytes 8 | tf_op jit(solution)/shard_map/psum | solution.py:43
  187.0 7.5 %psum.30 = f32[]{:T(128)} all-reduce(f32[]{:T(128)} %psum.29), channel_id=1, replica_groups=mesh['px_0'=4,'px_1'=4,'py_0'=4,'py_1'=2] {'py_0'}, use_global_device_ids=true, to_apply=%region_3.4 | all-reduce | flops 1 | bytes 8 | tf_op jit(solution)/shard_map/psum | solution.py:43
  195.5 9.2 %psum.31 = f32[]{:T(128)} all-reduce(f32[]{:T(128)} %psum.30), channel_id=1, replica_groups=mesh['px_0'=4,'px_1'=4,'py_0'=4,'py_1'=2] {'py_1'}, use_global_device_ids=true, to_apply=%region_4.5 | all-reduce | flops 1 | bytes 8 | tf_op jit(solution)/shard_map/psum | solution.py:43
  214.2 7.0 %all-to-all-done.8 = f32[128,1,256]{2,1,0:T(1,128)S(1)} async-done(((f32[128,1,256]{2,1,0:T(1,128)}), f32[128,1,256]{2,1,0:T(1,128)S(1)}, u32[]{:S(2)}, u32[]{:S(2)}) %all-to-all-start.8) | async-done | bytes 131104 | tf_op jit(solution)/shard_map/all_to_all | solution.py:36
  228.9 6.4 %all-to-all-done.9 = f32[128,1,256]{2,1,0:T(1,128)S(1)} async-done(((f32[128,1,256]{2,1,0:T(1,128)}), f32[128,1,256]{2,1,0:T(1,128)S(1)}, u32[]{:S(2)}, u32[]{:S(2)}) %all-to-all-start.9) | async-done | bytes 131104 | tf_op jit(solution)/shard_map/all_to_all | solution.py:36
  255.7 7.6 %all-to-all-done.10 = f32[128,1,256]{2,1,0:T(1,128)S(1)} async-done(((f32[128,1,256]{2,1,0:T(1,128)}), f32[128,1,256]{2,1,0:T(1,128)S(1)}, u32[]{:S(2)}, u32[]{:S(2)}) %all-to-all-start.10) | async-done | bytes 131104 | tf_op jit(solution)/shard_map/all_to_all | solution.py:36
  263.3 4.9 %all-to-all-start.11 = ((f32[128,1,256]{2,1,0:T(1,128)}), f32[128,1,256]{2,1,0:T(1,128)}, u32[]{:S(2)}, u32[]{:S(2)}) async-start(f32[128,1,256]{2,1,0:T(1,128)} %reshape.1419), calls=%async_computation.11 | async-start | bytes 262144 | tf_op jit(solution)/shard_map/all_to_all | solution.py:36
  271.6 6.4 %all-to-all-done.11 = f32[128,1,256]{2,1,0:T(1,128)} async-done(((f32[128,1,256]{2,1,0:T(1,128)}), f32[128,1,256]{2,1,0:T(1,128)}, u32[]{:S(2)}, u32[]{:S(2)}) %all-to-all-start.11) | async-done | bytes 131104 | tf_op jit(solution)/shard_map/all_to_all | solution.py:36
  296.4 7.5 %all-to-all-done.12 = f32[128,1,256]{2,1,0:T(1,128)S(1)} async-done(((f32[128,1,256]{2,1,0:T(1,128)}), f32[128,1,256]{2,1,0:T(1,128)S(1)}, u32[]{:S(2)}, u32[]{:S(2)}) %all-to-all-start.12) | async-done | bytes 131104 | tf_op jit(solution)/shard_map/all_to_all | solution.py:36
  311.8 6.5 %all-to-all-done.13 = f32[128,1,256]{2,1,0:T(1,128)S(1)} async-done(((f32[128,1,256]{2,1,0:T(1,128)}), f32[128,1,256]{2,1,0:T(1,128)S(1)}, u32[]{:S(2)}, u32[]{:S(2)}) %all-to-all-start.13) | async-done | bytes 131104 | tf_op jit(solution)/shard_map/all_to_all | solution.py:36
  337.9 7.4 %all-to-all-done.14 = f32[128,1,256]{2,1,0:T(1,128)S(1)} async-done(((f32[128,1,256]{2,1,0:T(1,128)}), f32[128,1,256]{2,1,0:T(1,128)S(1)}, u32[]{:S(2)}, u32[]{:S(2)}) %all-to-all-start.14) | async-done | bytes 131104 | tf_op jit(solution)/shard_map/all_to_all | solution.py:36
  353.0 6.6 %all-to-all-done.15 = f32[128,1,256]{2,1,0:T(1,128)S(1)} async-done(((f32[128,1,256]{2,1,0:T(1,128)}), f32[128,1,256]{2,1,0:T(1,128)S(1)}, u32[]{:S(2)}, u32[]{:S(2)}) %all-to-all-start.15) | async-done | bytes 131104 | tf_op jit(solution)/shard_map/all_to_all | solution.py:36
  (349 shorter events, 193.4 us)
Async XLA Ops:
  5.6 21.5 %all-to-all-start = ((f32[128,1,256]{2,1,0:T(1,128)}), f32[128,1,256]{2,1,0:T(1,128)S(1)}, u32[]{:S(2)}, u32[]{:S(2)}) async-start(f32[128,1,256]{2,1,0:T(1,128)} %reshape.1397), calls=%async_computation | async-start | bytes 262144 | tf_op jit(solution)/shard_map/all_to_all | solution.py:36
  27.1 14.4 %all-to-all-start.1 = ((f32[128,1,256]{2,1,0:T(1,128)}), f32[128,1,256]{2,1,0:T(1,128)S(1)}, u32[]{:S(2)}, u32[]{:S(2)}) async-start(f32[128,1,256]{2,1,0:T(1,128)} %reshape.1399), calls=%async_computation.1 | async-start | bytes 262144 | tf_op jit(solution)/shard_map/all_to_all | solution.py:36
  54.8 14.3 %all-to-all-start.2 = ((f32[128,1,256]{2,1,0:T(1,128)}), f32[128,1,256]{2,1,0:T(1,128)S(1)}, u32[]{:S(2)}, u32[]{:S(2)}) async-start(f32[128,1,256]{2,1,0:T(1,128)} %reshape.1401), calls=%async_computation.2 | async-start | bytes 262144 | tf_op jit(solution)/shard_map/all_to_all | solution.py:36
  69.1 14.7 %all-to-all-start.3 = ((f32[128,1,256]{2,1,0:T(1,128)}), f32[128,1,256]{2,1,0:T(1,128)S(1)}, u32[]{:S(2)}, u32[]{:S(2)}) async-start(f32[128,1,256]{2,1,0:T(1,128)} %reshape.1403), calls=%async_computation.3 | async-start | bytes 262144 | tf_op jit(solution)/shard_map/all_to_all | solution.py:36
  94.0 14.3 %all-to-all-start.4 = ((f32[128,1,256]{2,1,0:T(1,128)}), f32[128,1,256]{2,1,0:T(1,128)S(1)}, u32[]{:S(2)}, u32[]{:S(2)}) async-start(f32[128,1,256]{2,1,0:T(1,128)} %reshape.1405), calls=%async_computation.4 | async-start | bytes 262144 | tf_op jit(solution)/shard_map/all_to_all | solution.py:36
  108.3 14.4 %all-to-all-start.5 = ((f32[128,1,256]{2,1,0:T(1,128)}), f32[128,1,256]{2,1,0:T(1,128)S(1)}, u32[]{:S(2)}, u32[]{:S(2)}) async-start(f32[128,1,256]{2,1,0:T(1,128)} %reshape.1407), calls=%async_computation.5 | async-start | bytes 262144 | tf_op jit(solution)/shard_map/all_to_all | solution.py:36
  128.8 0.9 copy-start.3
  128.8 1.0 copy-start.4
  128.8 1.1 copy-start.5
  135.5 14.7 %all-to-all-start.6 = ((f32[128,1,256]{2,1,0:T(1,128)}), f32[128,1,256]{2,1,0:T(1,128)S(1)}, u32[]{:S(2)}, u32[]{:S(2)}) async-start(f32[128,1,256]{2,1,0:T(1,128)} %reshape.1409), calls=%async_computation.6 | async-start | bytes 262144 | tf_op jit(solution)/shard_map/all_to_all | solution.py:36
  150.2 14.3 %all-to-all-start.7 = ((f32[128,1,256]{2,1,0:T(1,128)}), f32[128,1,256]{2,1,0:T(1,128)S(1)}, u32[]{:S(2)}, u32[]{:S(2)}) async-start(f32[128,1,256]{2,1,0:T(1,128)} %reshape.1411), calls=%async_computation.7 | async-start | bytes 262144 | tf_op jit(solution)/shard_map/all_to_all | solution.py:36
  169.1 0.9 copy-start.6
  170.0 0.7 copy-start.2
  207.2 13.9 %all-to-all-start.8 = ((f32[128,1,256]{2,1,0:T(1,128)}), f32[128,1,256]{2,1,0:T(1,128)S(1)}, u32[]{:S(2)}, u32[]{:S(2)}) async-start(f32[128,1,256]{2,1,0:T(1,128)} %reshape.1413), calls=%async_computation.8 | async-start | bytes 262144 | tf_op jit(solution)/shard_map/all_to_all | solution.py:36
  221.1 14.2 %all-to-all-start.9 = ((f32[128,1,256]{2,1,0:T(1,128)}), f32[128,1,256]{2,1,0:T(1,128)S(1)}, u32[]{:S(2)}, u32[]{:S(2)}) async-start(f32[128,1,256]{2,1,0:T(1,128)} %reshape.1415), calls=%async_computation.9 | async-start | bytes 262144 | tf_op jit(solution)/shard_map/all_to_all | solution.py:36
  242.0 0.7 copy-start
  249.1 14.2 %all-to-all-start.10 = ((f32[128,1,256]{2,1,0:T(1,128)}), f32[128,1,256]{2,1,0:T(1,128)S(1)}, u32[]{:S(2)}, u32[]{:S(2)}) async-start(f32[128,1,256]{2,1,0:T(1,128)} %reshape.1417), calls=%async_computation.10 | async-start | bytes 262144 | tf_op jit(solution)/shard_map/all_to_all | solution.py:36
  263.3 14.7 %all-to-all-start.11 = ((f32[128,1,256]{2,1,0:T(1,128)}), f32[128,1,256]{2,1,0:T(1,128)}, u32[]{:S(2)}, u32[]{:S(2)}) async-start(f32[128,1,256]{2,1,0:T(1,128)} %reshape.1419), calls=%async_computation.11 | async-start | bytes 262144 | tf_op jit(solution)/shard_map/all_to_all | solution.py:36
  289.4 14.5 %all-to-all-start.12 = ((f32[128,1,256]{2,1,0:T(1,128)}), f32[128,1,256]{2,1,0:T(1,128)S(1)}, u32[]{:S(2)}, u32[]{:S(2)}) async-start(f32[128,1,256]{2,1,0:T(1,128)} %reshape.1421), calls=%async_computation.12 | async-start | bytes 262144 | tf_op jit(solution)/shard_map/all_to_all | solution.py:36
  303.9 14.4 %all-to-all-start.13 = ((f32[128,1,256]{2,1,0:T(1,128)}), f32[128,1,256]{2,1,0:T(1,128)S(1)}, u32[]{:S(2)}, u32[]{:S(2)}) async-start(f32[128,1,256]{2,1,0:T(1,128)} %reshape.1423), calls=%async_computation.13 | async-start | bytes 262144 | tf_op jit(solution)/shard_map/all_to_all | solution.py:36
  324.3 1.0 copy-start.1
  330.8 14.5 %all-to-all-start.14 = ((f32[128,1,256]{2,1,0:T(1,128)}), f32[128,1,256]{2,1,0:T(1,128)S(1)}, u32[]{:S(2)}, u32[]{:S(2)}) async-start(f32[128,1,256]{2,1,0:T(1,128)} %reshape.1425), calls=%async_computation.14 | async-start | bytes 262144 | tf_op jit(solution)/shard_map/all_to_all | solution.py:36
  345.3 14.3 %all-to-all-start.15 = ((f32[128,1,256]{2,1,0:T(1,128)}), f32[128,1,256]{2,1,0:T(1,128)S(1)}, u32[]{:S(2)}, u32[]{:S(2)}) async-start(f32[128,1,256]{2,1,0:T(1,128)} %reshape.1427), calls=%async_computation.15 | async-start | bytes 262144 | tf_op jit(solution)/shard_map/all_to_all | solution.py:36
where the time goes:
time: 373 us; the launch traced here: 366 us
  waiting for transfers between devices  110 us (29%)
  starting transfers between devices  78.2 us (21%)
  local copies, waits for them, and re-layouts  67.6 us (18%)
  matrix products  54.7 us (15%)
  blocking collectives  31.4 us (8%)
  other arithmetic  18.9 us (5%)
  between operations  5.73 us (2%)
    all_to_all x16, waiting for transfers between devices, one_exchange(): tiles = lax.all_to_all(tiles, axis, split_axis=0, concat_axis=0, tiled=True)  110 us
    all_to_all x16, starting transfers between devices, one_exchange(): tiles = lax.all_to_all(tiles, axis, split_axis=0, concat_axis=0, tiled=True)  78.2 us
    psum x4, blocking collectives, one_axis_at_a_time(): shard = lax.psum(shard, axis)  31.4 us
    unnamed x46, local copies, waits for them, and re-layouts  24.8 us
    all_to_all x16, other arithmetic, one_exchange(): tiles = lax.all_to_all(tiles, axis, split_axis=0, concat_axis=0, tiled=True)  16.8 us
    reshape x16, local copies, waits for them, and re-layouts, one_exchange(): tiles = laid_out(tiles.reshape(*sizes, *inside), concats[0] + 1)  14.1 us
    dot_general x29, matrix products, complex_einsum(): imag_term = jnp.einsum(formula, left_real, table_pair[1], precision=highest)  13.6 us
    dot_general x29, matrix products, complex_einsum(): real_term = jnp.einsum(formula, left_real, table_pair[0], precision=highest)  13.5 us
  transfers between devices with their start and end apart: 16, of which 16 were waited for; matrix products, arithmetic and copies ran while one was open for 13% of the time, Pallas kernels for 0%

commit v1 on v0

--- a/solution.py
+++ b/solution.py
@@ -3,12 +3,13 @@
 import jax
 import jax.numpy as jnp
 from jax import lax
-from jax.sharding import Mesh
+from jax.experimental import pallas as pl
+from jax.experimental.pallas import tpu as pltpu
 from jax.sharding import PartitionSpec as P
 
-PX_PY = ("px_0", "px_1", "py_0", "py_1")
-PX = ("px_0", "px_1")
-PY = ("py_0", "py_1")
+PX_PY = ("px", "py")
+PX = "px"
+PY = "py"
 
 
 time_step = 0.25
@@ -25,6 +26,60 @@
     tiles = jnp.moveaxis(tiles, 0, dim)
     dims = tiles.shape
     return tiles.reshape(*dims[:dim], dims[dim] * dims[dim + 1], *dims[dim + 2 :])
+
+
+MESH = pl.DeviceIdType.MESH
+peers = 128
+
+
+def swap_kernel(x_ref, o_ref, recv, send_sem, recv_sem, own_sem):
+    me = lax.axis_index("px") * 8 + lax.axis_index("py")
+    barrier = pltpu.get_barrier_semaphore()
+
+    def greet(i, carry):
+        d = jnp.bitwise_xor(me, i)
+        pl.semaphore_signal(barrier, inc=1, device_id=(d // 8, d % 8), device_id_type=MESH)
+        return carry
+
+    lax.fori_loop(1, peers, greet, 0)
+    pl.semaphore_wait(barrier, peers - 1)
+    own = pltpu.make_async_copy(x_ref.at[me], recv.at[me], own_sem)
+    own.start()
+
+    def send(i, carry):
+        d = jnp.bitwise_xor(me, peers - i)
+        pltpu.make_async_remote_copy(
+            x_ref.at[d], recv.at[me], send_sem, recv_sem,
+            device_id=(d // 8, d % 8), device_id_type=MESH,
+        ).start()
+        return carry
+
+    lax.fori_loop(1, peers, send, 0)
+    own.wait()
+    whole = pltpu.make_async_remote_copy(
+        x_ref.at[pl.ds(0, peers - 1)], recv.at[pl.ds(0, peers - 1)], send_sem, recv_sem,
+        device_id=(0, 0), device_id_type=MESH,
+    )
+    whole.wait_recv()
+    whole.wait_send()
+    o_ref[...] = recv[...]
+
+
+def swap(x):
+    shape = (peers, 2, 128)
+    return pl.pallas_call(
+        swap_kernel,
+        out_shape=jax.ShapeDtypeStruct(shape, jnp.float32),
+        in_specs=[pl.BlockSpec(memory_space=pltpu.VMEM)],
+        out_specs=pl.BlockSpec(memory_space=pltpu.VMEM),
+        scratch_shapes=[
+            pltpu.VMEM(shape, jnp.float32),
+            pltpu.SemaphoreType.DMA,
+            pltpu.SemaphoreType.DMA,
+            pltpu.SemaphoreType.DMA,
+        ],
+        compiler_params=pltpu.CompilerParams(collective_id=0, has_side_effects=True),
+    )(x)
 
 
 def one_exchange(shard, axis, axes, splits, concats):
@@ -33,7 +88,7 @@
     tiles = jnp.moveaxis(in_blocks(tiles, splits[1] + 1, sizes[1]), 0, 1)
     inside = tiles.shape[2:]
     tiles = tiles.reshape(-1, *inside)
-    tiles = lax.all_to_all(tiles, axis, split_axis=0, concat_axis=0, tiled=True)
+    tiles = swap(tiles.reshape(128, 2, 128)).reshape(tiles.shape)
     tiles = laid_out(tiles.reshape(*sizes, *inside), concats[0] + 1)
     return laid_out(tiles, concats[1])
 
@@ -185,9 +240,8 @@
 
 
 def solution(mesh):
-    finer = Mesh(mesh.devices.reshape(4, 4, 4, 2), ("px_0", "px_1", "py_0", "py_1"))
     in_specs = (P(None, PX_PY, None), P(None, PX_PY, None), P(None, PX_PY, None))
     out_specs = (P(None, PX_PY, None), P(), P(None, PX_PY, None), P(None, PX_PY, None))
     return jax.shard_map(
-        per_device, mesh=finer, in_specs=in_specs, out_specs=out_specs, check_vma=False
-    )
+        per_device, mesh=mesh, in_specs=in_specs, out_specs=out_specs, check_vma=False
+    )

time: 373 us -> 413 us (1.11)
  Pallas kernels: 0 us -> 224 us
  waiting for transfers between devices: 110 us -> 0 us
  starting transfers between devices: 78.2 us -> 0 us
  blocking collectives: 31.4 us -> 52.2 us
  other arithmetic: 18.9 us -> 2.05 us
    pallas_call x0 -> x16, Pallas kernels: none -> 224 us  [swap(): pl.pallas_call(swap_kernel, out_shape=jax.ShapeDtypeStruct(shape, jnp.flo...]
    all_to_all x16 -> x0, waiting for transfers between devices: 110 us -> none  [one_exchange(): tiles = lax.all_to_all(tiles, axis, split_axis=0, concat_axis=0, tiled=True)]
    all_to_all x16 -> x0, starting transfers between devices: 78.2 us -> none  [one_exchange(): tiles = lax.all_to_all(tiles, axis, split_axis=0, concat_axis=0, tiled=True)]
    another operation x19 -> x51, local copies, waits for them, and re-layouts: 4.79 us -> 44.3 us  [the longest x16 20.5 us: one_exchange(): tiles = laid_out(tiles.reshape(*sizes, *inside), concats[0] + 1)]
    unnamed x46 -> x16, local copies, waits for them, and re-layouts: 24.8 us -> 3.36 us
    psum x4 -> x2, blocking collectives: 31.4 us -> 52.2 us  [one_axis_at_a_time(): shard = lax.psum(shard, axis)]
    all_to_all x16 -> x0, other arithmetic: 16.8 us -> none  [one_exchange(): tiles = lax.all_to_all(tiles, axis, split_axis=0, concat_axis=0, tiled=True)]
    reshape x17 -> x1, local copies, waits for them, and re-layouts: 15.1 us -> 0.1 us  [the longest x16 14.1 us: one_exchange(): tiles = laid_out(tiles.reshape(*sizes, *inside), concats[0] + 1)]
  transfers between devices with their start and end apart: 16 -> 0, of which waited for: 16 -> 0; matrix products, arithmetic and copies ran while one was open for 13% -> 0% of each run, Pallas kernels for 0% -> 0%
where the time goes in v1:
time: 413 us; the launch traced here: 408 us
  Pallas kernels  224 us (54%)
  local copies, waits for them, and re-layouts  70.2 us (17%)
  matrix products  54.7 us (13%)
  blocking collectives  52.2 us (13%)
  between operations  5.4 us (1%)
    pallas_call x16, Pallas kernels, swap(): pl.pallas_call(swap_kernel, out_shape=jax.ShapeDtypeStruct(shape, jnp.flo...  224 us
    psum x2, blocking collectives, one_axis_at_a_time(): shard = lax.psum(shard, axis)  52.2 us
    another operation x16, local copies, waits for them, and re-layouts, one_exchange(): tiles = laid_out(tiles.reshape(*sizes, *inside), concats[0] + 1)  20.5 us
    another operation x16, local copies, waits for them, and re-layouts, one_exchange(): tiles = swap(tiles.reshape(128, 2, 128)).reshape(tiles.shape)  17.7 us
    dot_general x29, matrix products, complex_einsum(): imag_term = jnp.einsum(formula, left_real, table_pair[1], precision=highest)  13.6 us
    dot_general x29, matrix products, complex_einsum(): real_term = jnp.einsum(formula, left_real, table_pair[0], precision=highest)  13.5 us
    dot_general x26, matrix products, complex_einsum(): jnp.einsum(formula, left_imag, table_pair[1], precision=highest)  12.3 us
    dot_general x26, matrix products, complex_einsum(): jnp.einsum(formula, left_imag, table_pair[0], precision=highest)  12.3 us

profile of v1, /device:TPU:1, one launch (start us, length us, event | category | flops | bytes accessed | tf_op | source)
XLA Modules:
  0.0 408.5 jit_solution(14829458096364494532)
XLA Ops:
  7.1 19.4 %shard_map.66 = f32[128,2,128]{2,1,0:T(2,128)} custom-call(f32[128,2,128]{2,1,0:T(2,128)} %reshape_reshape.161.x_ref), custom_call_target="tpu_custom_call" | custom-call | tf_op jit(solution)/shard_map/pallas_call | solution.py:70
  26.4 1.3 reshape_reshape.162
  30.6 13.5 %shard_map.67 = f32[128,2,128]{2,1,0:T(2,128)} custom-call(f32[128,2,128]{2,1,0:T(2,128)} %reshape_reshape.164.x_ref), custom_call_target="tpu_custom_call" | custom-call | tf_op jit(solution)/shard_map/pallas_call | solution.py:70
  44.1 1.3 reshape_reshape.165
  56.9 14.0 %shard_map.68 = f32[128,2,128]{2,1,0:T(2,128)} custom-call(f32[128,2,128]{2,1,0:T(2,128)} %reshape_reshape.167.x_ref), custom_call_target="tpu_custom_call" | custom-call | tf_op jit(solution)/shard_map/pallas_call | solution.py:70
  70.9 1.3 reshape_reshape.168
  75.0 13.5 %shard_map.69 = f32[128,2,128]{2,1,0:T(2,128)} custom-call(f32[128,2,128]{2,1,0:T(2,128)} %reshape_reshape.170.x_ref), custom_call_target="tpu_custom_call" | custom-call | tf_op jit(solution)/shard_map/pallas_call | solution.py:70
  88.5 1.3 reshape_reshape.171
  98.9 13.9 %shard_map.70 = f32[128,2,128]{2,1,0:T(2,128)} custom-call(f32[128,2,128]{2,1,0:T(2,128)} %reshape_reshape.173.x_ref), custom_call_target="tpu_custom_call" | custom-call | tf_op jit(solution)/shard_map/pallas_call | solution.py:70
  116.9 13.4 %shard_map.71 = f32[128,2,128]{2,1,0:T(2,128)} custom-call(f32[128,2,128]{2,1,0:T(2,128)} %reshape_reshape.176.x_ref), custom_call_target="tpu_custom_call" | custom-call | tf_op jit(solution)/shard_map/pallas_call | solution.py:70
  143.3 13.8 %shard_map.72 = f32[128,2,128]{2,1,0:T(2,128)} custom-call(f32[128,2,128]{2,1,0:T(2,128)} %reshape_reshape.179.x_ref), custom_call_target="tpu_custom_call" | custom-call | tf_op jit(solution)/shard_map/pallas_call | solution.py:70
  161.3 13.5 %shard_map.73 = f32[128,2,128]{2,1,0:T(2,128)} custom-call(f32[128,2,128]{2,1,0:T(2,128)} %reshape_reshape.182.x_ref), custom_call_target="tpu_custom_call" | custom-call | tf_op jit(solution)/shard_map/pallas_call | solution.py:70
  180.8 32.1 %psum.14 = f32[]{:T(128)} all-reduce(f32[]{:T(128)S(6)} %mul_shard_map.3), channel_id=1, replica_groups=mesh['px'=16,'py'=8] {'px'}, use_global_device_ids=true, to_apply=%region_1.2 | all-reduce | flops 1 | bytes 8 | tf_op jit(solution)/shard_map/psum | solution.py:98
  212.9 20.0 %psum.15 = f32[]{:T(128)} all-reduce(f32[]{:T(128)} %psum.14), channel_id=1, replica_groups=mesh['px'=16,'py'=8] {'py'}, use_global_device_ids=true, to_apply=%region_2.3 | all-reduce | flops 1 | bytes 8 | tf_op jit(solution)/shard_map/psum | solution.py:98
  239.1 13.4 %shard_map.74 = f32[128,2,128]{2,1,0:T(2,128)} custom-call(f32[128,2,128]{2,1,0:T(2,128)} %reshape_reshape.185.x_ref), custom_call_target="tpu_custom_call" | custom-call | tf_op jit(solution)/shard_map/pallas_call | solution.py:70
  256.7 13.9 %shard_map.75 = f32[128,2,128]{2,1,0:T(2,128)} custom-call(f32[128,2,128]{2,1,0:T(2,128)} %reshape_reshape.188.x_ref), custom_call_target="tpu_custom_call" | custom-call | tf_op jit(solution)/shard_map/pallas_call | solution.py:70
  284.4 13.6 %shard_map.76 = f32[128,2,128]{2,1,0:T(2,128)} custom-call(f32[128,2,128]{2,1,0:T(2,128)} %reshape_reshape.191.x_ref), custom_call_target="tpu_custom_call" | custom-call | tf_op jit(solution)/shard_map/pallas_call | solution.py:70
  302.7 13.6 %shard_map.77 = f32[128,2,128]{2,1,0:T(2,128)} custom-call(f32[128,2,128]{2,1,0:T(2,128)} %reshape_reshape.194.x_ref), custom_call_target="tpu_custom_call" | custom-call | tf_op jit(solution)/shard_map/pallas_call | solution.py:70
  316.4 1.3 reshape_reshape.195
  327.0 13.6 %shard_map.78 = f32[128,2,128]{2,1,0:T(2,128)} custom-call(f32[128,2,128]{2,1,0:T(2,128)} %reshape_reshape.197.x_ref), custom_call_target="tpu_custom_call" | custom-call | tf_op jit(solution)/shard_map/pallas_call | solution.py:70
  344.8 13.7 %shard_map.79 = f32[128,2,128]{2,1,0:T(2,128)} custom-call(f32[128,2,128]{2,1,0:T(2,128)} %reshape_reshape.200.x_ref), custom_call_target="tpu_custom_call" | custom-call | tf_op jit(solution)/shard_map/pallas_call | solution.py:70
  358.5 1.3 reshape_reshape.201
  371.1 13.7 %shard_map.80 = f32[128,2,128]{2,1,0:T(2,128)} custom-call(f32[128,2,128]{2,1,0:T(2,128)} %reshape_reshape.203.x_ref), custom_call_target="tpu_custom_call" | custom-call | tf_op jit(solution)/shard_map/pallas_call | solution.py:70
  388.9 13.6 %shard_map.81 = f32[128,2,128]{2,1,0:T(2,128)} custom-call(f32[128,2,128]{2,1,0:T(2,128)} %reshape_reshape.206.x_ref), custom_call_target="tpu_custom_call" | custom-call | tf_op jit(solution)/shard_map/pallas_call | solution.py:70
  (300 shorter events, 119.3 us)
Async XLA Ops:
  0.6 0.9 copy-start.6
  135.6 0.9 copy-start.4
  135.7 1.0 copy-start.5
  178.6 0.9 copy-start.7
  179.5 0.7 copy-start.2
  276.3 1.9 copy-start
  300.2 0.9 copy-start.3
  363.6 1.0 copy-start.1

commit v2 on v0

v2 whole, which is shorter than its diff:
```python
import math

import jax
import jax.numpy as jnp
import numpy as np
from jax import lax
from jax.experimental import pallas as pl
from jax.experimental.pallas import tpu as pltpu
from jax.sharding import PartitionSpec as P

MESH = pl.DeviceIdType.MESH
f32 = jnp.float32
bf16 = jnp.bfloat16

n = 2048
peers = 128
step = 0.25
unit = 4.0 / n
half_rows = 72


def cplx(table):
    return np.block([[table.real, table.imag], [-table.imag, table.real]])


def signed(count, index):
    return np.where(index < count // 2, index, index - count)


def build_tables():
    s = np.arange(128)
    a1 = np.arange(65)
    theta = 2 * np.pi * np.outer(a1, s) / 128
    td = np.zeros((2 * half_rows, 128))
    td[:65] = np.cos(theta)
    td[half_rows : half_rows + 65] = -np.sin(theta)
    weight = np.where((a1 == 0) | (a1 == 64), 1.0, 2.0) / 128
    ti = np.zeros((128, 2 * half_rows))
    ti[:, :65] = (np.cos(theta) * weight[:, None]).T
    ti[:, half_rows : half_rows + 65] = (-np.sin(theta) * weight[:, None]).T

    def derivative(length, factor):
        freq = signed(length, s[:length]).astype(float) * factor
        inner = np.where(s[:length] == length // 2, 0.0, freq)
        gap = np.subtract.outer(s[:length], s[:length])
        waves = np.exp(2j * np.pi * gap[:, :, None] * s[:length] / length)
        smooth = (waves * (1j * inner)).sum(-1).real / length
        nyquist = freq[length // 2] * (-1.0) ** gap / length
        return (smooth + 1j * nyquist).T

    root = 1.0 / math.sqrt(n)
    mx = cplx(np.kron(np.eye(8), derivative(16, unit * 128)))
    my = cplx(derivative(128, unit * 16) / 16)

    w16 = np.exp(-2j * np.pi * np.outer(s[:16], s[:16]) / 16)
    eye8 = np.eye(8)
    forward = w16.reshape(16, 2, 8)
    parts = np.zeros((2, 8, 16, 2, 2, 8, 8))
    for y in range(8):
        parts[0, y, :, :, 0, :, y] = forward.real
        parts[0, y, :, :, 1, :, y] = forward.imag
        parts[1, y, :, :, 0, :, y] = -forward.imag
        parts[1, y, :, :, 1, :, y] = forward.real
    wx = parts.reshape(256, 256) * root
    back = w16.conj().T.reshape(2, 8, 16)
    parts = np.zeros((2, 2, 8, 8, 2, 8, 16))
    for y in range(8):
        parts[:, 0, :, y, 0, y, :] = back.real
        parts[:, 0, :, y, 1, y, :] = back.imag
        parts[:, 1, :, y, 0, y, :] = -back.imag
        parts[:, 1, :, y, 1, y, :] = back.real
    wxi = parts.reshape(256, 256) * (128 * root)
    forward = w16.reshape(2, 8, 16)
    parts = np.zeros((2, 2, 8, 8, 2, 2, 8, 16))
    for k in range(8):
        for c in range(2):
            parts[:, c, k, :, c, 0, k, :] = forward.real
            parts[:, c, k, :, c, 1, k, :] = forward.imag
    wy = parts.reshape(256, 512)
    back = w16.conj().T.reshape(16, 2, 8)
    parts = np.zeros((2, 8, 16, 2, 2, 8, 8))
    for k in range(8):
        parts[0, k, :, :, 0, k, :] = back.real
        parts[0, k, :, :, 1, k, :] = back.imag
        parts[1, k, :, :, 0, k, :] = -back.imag
        parts[1, k, :, :, 1, k, :] = back.real
    wyi = parts.reshape(256, 256)
    f128 = np.exp(-2j * np.pi * np.outer(s, s) / 128) * root
    ty = cplx(f128).T
    tyi = cplx(f128.conj()).T
    squares = np.stack([mx, my, wx, wxi, wy[:, :256], wy[:, 256:], wyi, ty, tyi])

    own = np.zeros((128, 2, 128))
    mirror = np.zeros((128, 2, 128))
    for e in range(128):
        h, a = e % 2, e // 2
        if e == 0:
            own[e, 0, 0] = mirror[e, 1, 0] = 1
        elif e == 1:
            own[e, 0, 64] = mirror[e, 1, 64] = 1
        else:
            own[e, h, a] = mirror[e, 1 - h, 128 - a] = 1
    places = np.stack([own.reshape(128, 256), mirror.reshape(128, 256)])

    row = np.arange(half_rows)[:, None]
    lane = np.arange(128)[None, :]
    twx = 2 * np.pi * row * (lane % 16) / n
    twy = 2 * np.pi * np.arange(128)[:, None] * (lane % 16) / n
    twr = 2 * np.pi * np.arange(16)[:, None] * lane / n
    both = lambda t: np.stack([np.cos(t), np.sin(t)]).astype(np.float32)

    def halves(t):
        high = t.astype(np.float32).astype(bf16)
        low = (t - high.astype(np.float64)).astype(np.float32).astype(bf16)
        return high, low

    return dict(
        squares=np.stack(halves(squares), axis=1),
        td=np.stack(halves(td)),
        ti=np.stack(halves(ti)),
        places=places.astype(np.float32).astype(bf16),
        places_t=places.transpose(0, 2, 1).astype(np.float32).astype(bf16),
        twx=both(twx),
        twy=both(twy),
        twr=both(twr),
    )


MX, MY, WX, WXI, WYA, WYB, WYI, TY, TYI = range(9)
NAMES = ("squares", "td", "ti", "places", "places_t", "twx", "twy", "twr")


def split(x):
    high = x.astype(bf16)
    return high, (x - high.astype(f32)).astype(bf16)


def dot(a, b):
    return jnp.dot(a, b, preferred_element_type=f32)


def product(a, b):
    return dot(a[0], b[0]) + (dot(a[0], b[1]) + dot(a[1], b[0]))


def left(table, x):
    return product((table[0], table[1]), split(x))


def right(x, table):
    return product(split(x), (table[0], table[1]))


def cat(parts, axis):
    return jnp.concatenate(parts, axis=axis)


def turn(re, im, cos, sin):
    return re * cos + im * sin, im * cos - re * sin


def turn_back(re, im, cos, sin):
    return re * cos - im * sin, im * cos + re * sin


def real_dft(values):
    count = len(values)
    if count == 2:
        return [(values[0] + values[1], None), (values[0] - values[1], None)]
    even, odd = real_dft(values[0::2]), real_dft(values[1::2])
    quarter = count // 4
    out = [None] * (count // 2 + 1)
    for k in range(quarter + 1):
        (er, ei), (tr, ti) = even[k], odd[k]
        if k == quarter:
            out[k] = (er, -tr)
            continue
        if k > 0:
            c, s = math.cos(2 * math.pi * k / count), math.sin(2 * math.pi * k / count)
            tr, ti = (tr * c + ti * s, ti * c - tr * s) if ti is not None else (tr * c, tr * -s)
        if k == 0:
            out[0], out[count // 2] = (er + tr, None), (er - tr, None)
        else:
            ei = 0.0 if ei is None else ei
            out[k] = (er + tr, ei + ti)
            out[count // 2 - k] = (er - tr, ti - ei)
    return out


def real_idft(spectrum):
    count = 2 * (len(spectrum) - 1)
    if count == 2:
        return [spectrum[0][0] + spectrum[1][0], spectrum[0][0] - spectrum[1][0]]
    quarter = count // 4
    even, odd = [], []
    for k in range(quarter + 1):
        re, im = spectrum[k]
        if k == 0:
            other = spectrum[count // 2][0]
            even.append((re + other, None))
            odd.append((re - other, None))
        elif k == quarter:
            even.append((2.0 * re, None))
            odd.append((-2.0 * im, None))
        else:
            hr, hi = spectrum[count // 2 - k]
            even.append((re + hr, im - hi))
            dr, di = re - hr, im + hi
            c, s = math.cos(2 * math.pi * k / count), math.sin(2 * math.pi * k / count)
            odd.append((dr * c - di * s, dr * s + di * c))
    xs, ys = real_idft(even), real_idft(odd)
    return [v for pair in zip(xs, ys) for v in pair]


def rows_derivative(tiles, t):
    cos, sin = t["twr"][0], t["twr"][1]
    turned = []
    for k, (re, im) in enumerate(real_dft(tiles)):
        c, s = cos[k : k + 1], sin[k : k + 1]
        if k == 0:
            turned.append((re, jnp.zeros_like(re)))
        elif im is None:
            turned.append((re * c, -re * s))
        else:
            turned.append(turn(re, im, c, s))
    re_rows = cat([v[0] for v in turned], 0)
    im_rows = cat([v[1] for v in turned], 0)
    moved = right(cat([re_rows, im_rows], 1), t["squares"][MY])
    out = []
    for k, (re, im) in enumerate(turned):
        mr = moved[16 * k : 16 * k + 16, :128] - (unit / 16 * k) * im
        mi = moved[16 * k : 16 * k + 16, 128:] + (unit / 16 * k) * re
        out.append(turn_back(mr, mi, cos[k : k + 1], sin[k : k + 1]))
    return real_idft(out)


def columns_half(x, t):
    y = left(t["td"], x)
    cos, sin = t["twx"][0], t["twx"][1]
    out = []
    for g in range(x.shape[1] // 128):
        part = y[:, 128 * g : 128 * g + 128]
        out.append(turn(part[:half_rows], part[half_rows:], cos, sin))
    return out


def columns_back(parts, t):
    cos, sin = t["twx"][0], t["twx"][1]
    cols = []
    for re, im in parts:
        br, bi = turn_back(re, im, cos, sin)
        cols.append(cat([br, bi], 0))
    return left(t["ti"], cat(cols, 1))


def columns_derivative(x, t):
    parts = columns_half(x, t)
    stacked = cat([cat([re, im], 1) for re, im in parts], 0)
    moved = right(stacked, t["squares"][MX])
    slope = unit * lax.broadcasted_iota(jnp.int32, (half_rows, 128), 0).astype(f32)
    out = []
    for g, (re, im) in enumerate(parts):
        rows = slice(half_rows * g, half_rows * (g + 1))
        out.append((moved[rows, :128] - slope * im, moved[rows, 128:] + slope * re))
    return columns_back(out, t)


def columns_spectrum(x, t):
    parts = columns_half(x, t)
    stacked = cat([cat([re, im], 1) for re, im in parts], 0)
    z = right(stacked, t["squares"][WX])
    row = lax.broadcasted_iota(jnp.int32, (8, 128), 0)
    lane = lax.broadcasted_iota(jnp.int32, (8, 128), 1)
    slot = (row == 0) & (lane >= 64) & (lane < 72)
    out = []
    for g in range(len(parts)):
        base = half_rows * g
        z0, z1 = z[base : base + half_rows, :128], z[base : base + half_rows, 128:]
        top0 = jnp.where(slot, roll(z1[:8], 64), z0[:8])
        top1 = jnp.where(row == 0, z0[64:72], z1[:8])
        out.append((cat([top0, z0[8:64]], 0), cat([top1, z1[8:64]], 0)))
    return out


def columns_field(blocks, t):
    row = lax.broadcasted_iota(jnp.int32, (8, 128), 0)
    lane = lax.broadcasted_iota(jnp.int32, (8, 128), 1)
    first = jnp.where(lane < 8, 1.0, jnp.where((lane >= 64) & (lane < 72), 0.0, 2.0))
    stacked = []
    for x0, x1 in blocks:
        top0 = jnp.where(row == 0, first * x0[:8], x0[:8])
        kept = jnp.where(lane < 8, roll(x0[:8], 64), 0.0)
        top1 = jnp.where(row == 0, kept, x1[:8])
        last0 = jnp.where(row == 0, 2.0 * x1[:8], 0.0)
        stacked.append(
            cat(
                [
                    cat([top0, x0[8:], last0], 0),
                    cat([top1, x1[8:], jnp.zeros_like(last0)], 0),
                ],
                1,
            )
        )
    z = right(cat(stacked, 0), t["squares"][WXI])
    parts = []
    for g in range(len(blocks)):
        rows = slice(half_rows * g, half_rows * (g + 1))
        parts.append((z[rows, :128], z[rows, 128:]))
    return columns_back(parts, t)


def waves_forward(x, t):
    blocks = x.shape[0] // 128
    cos, sin = t["twy"][0], t["twy"][1]
    halves = split(x)
    lanes = []
    for table in (WYA, WYB):
        y = product(halves, (t["squares"][table][0], t["squares"][table][1]))
        for b in range(blocks):
            rows = slice(128 * b, 128 * b + 128)
            re, im = turn(y[rows, :128], y[rows, 128:], cos, sin)
            lanes.append(cat([re, im], 0))
    z = left(t["squares"][TY], cat(lanes, 1))
    out = []
    for b in range(blocks):
        for origin in range(2):
            at = 128 * (origin * blocks + b)
            out.append((z[:128, at : at + 128], z[128:, at : at + 128]))
    return out


def waves_back(values, t):
    cos, sin = t["twy"][0], t["twy"][1]
    z = left(t["squares"][TYI], cat([cat([re, im], 0) for re, im in values], 1))
    rows = []
    for v in range(len(values)):
        part = z[:, 128 * v : 128 * v + 128]
        rows.append(cat(turn_back(part[:128], part[128:], cos, sin), 1))
    y = right(cat(rows, 0), t["squares"][WYI])
    return [y[128 * v : 128 * v + 128] for v in range(len(values))]


def roll(x, shift):
    return pltpu.roll(x, shift, 1)


def denominators(me):
    lane = lax.broadcasted_iota(jnp.int32, (128, 128), 1)
    row = lax.broadcasted_iota(jnp.int32, (128, 128), 0)
    k = lane // 16
    first = jnp.where(me == 1, 64, me // 2) + 1024 * jnp.where(me == 1, 0, me % 2)
    a = first + 128 * k
    b = lane % 16 + 16 * row
    packed = (k == 0) & (me == 0)

    def square(index):
        wave = unit * jnp.where(index < n // 2, index, index - n).astype(f32)
        return wave * wave

    out = []
    for index in (a, jnp.where(packed, n // 2, a)):
        ksq = square(index) + square(b)
        out.append(1.0 / (1.0 + step * (ksq * ksq - ksq)))
    return out[0], out[1], packed


ROWS = dict(ug=4, t=2, f=4, wt=4, m=2, n=2, fg=4, q=2, v=2, nx=2)
KEYS = tuple(ROWS)


def kernel(*refs):
    u_ref, t_ref, f_ref = refs[:3]
    tables_hbm = refs[3 : 3 + len(NAMES)]
    refs = refs[3 + len(NAMES) :]
    next_ref, objective_ref, grad_ref, fgrad_ref = refs[:4]
    refs = refs[4:]
    tables = dict(zip(NAMES, refs[: len(NAMES)]))
    refs = refs[len(NAMES) :]
    send = dict(zip(KEYS, refs[: len(KEYS)]))
    refs = refs[len(KEYS) :]
    recv = dict(zip(KEYS, refs[: len(KEYS)]))
    refs = refs[len(KEYS) :]
    part_ref, parts_ref, g1_ref, g2_ref, forced_ref = refs[:5]
    table_sem, send_sem, recv_sem, own_sem = refs[5:]

    me = lax.axis_index("px") * 8 + lax.axis_index("py")
    barrier = pltpu.get_barrier_semaphore()

    def greet(i, carry):
        d = jnp.bitwise_xor(me, i)
        pl.semaphore_signal(barrier, inc=1, device_id=(d // 8, d % 8), device_id_type=MESH)
        return carry

    loads = [
        pltpu.make_async_copy(src, tables[name], table_sem.at[i])
        for i, (name, src) in enumerate(zip(NAMES, tables_hbm))
    ]
    for load in loads:
        load.start()
    lax.fori_loop(1, peers, greet, 0)

    def flat(ref):
        return ref.reshape(ref.shape[0] * ref.shape[1], 128)

    def put(key, row, value):
        flat(send[key])[pl.ds(row, peers, ROWS[key]), :] = value

    def get(key, row, count=peers, stride=None):
        return flat(recv[key])[pl.ds(row, count, stride or ROWS[key]), :]

    def start(key):
        i = KEYS.index(key)
        src, dst = send[key], recv[key]
        pltpu.make_async_copy(src.at[me], dst.at[me], own_sem.at[i]).start()

        def one(j, carry):
            d = jnp.bitwise_xor(me, peers - j)
            pltpu.make_async_remote_copy(
                src.at[d], dst.at[me], send_sem.at[i], recv_sem.at[i],
                device_id=(d // 8, d % 8), device_id_type=MESH,
            ).start()
            return carry

        lax.fori_loop(1, peers, one, 0)

    def whole(key):
        i = KEYS.index(key)
        span = pl.ds(0, peers - 1)
        return pltpu.make_async_remote_copy(
            send[key].at[span], recv[key].at[span], send_sem.at[i], recv_sem.at[i],
            device_id=(0, 0), device_id_type=MESH,
        )

    def arrive(key):
        i = KEYS.index(key)
        pltpu.make_async_copy(send[key].at[me], recv[key].at[me], own_sem.at[i]).wait()
        whole(key).wait_recv()

    def tiles_of(ref):
        return [ref[:, 128 * i : 128 * i + 128] for i in range(16)]

    def put_field(key, row, tiles):
        for g in range(2):
            put(key, row + g, cat(tiles[8 * g : 8 * g + 8], 0).T)

    def get_tiles(key):
        out = []
        for g in range(2):
            block = get(key, g).T
            out += [block[16 * i : 16 * i + 16] for i in range(8)]
        return out

    for load in loads:
        load.wait()
    t = tables
    u_tiles = tiles_of(u_ref)
    put_field("ug", 0, u_tiles)
    put_field("ug", 2, rows_derivative(u_tiles, t))
    put_field("t", 0, tiles_of(t_ref))
    pl.semaphore_wait(barrier, peers - 1)
    start("ug")
    start("t")
    for c in range(2):
        for which in range(2):
            sides = []
            for h in range(2):
                order = range(8) if which == 0 else range(7, -1, -1)
                sides.append(
                    cat([f_ref[c, :, 128 * (8 * h + k) : 128 * (8 * h + k) + 128] for k in order], 0)
                )
            high, low = split(cat(sides, 1))
            dims = (((1,), (1,)), ((), ()))
            place = t["places"][which]
            moved = lax.dot_general(place, high, dims, preferred_element_type=f32)
            moved = moved + lax.dot_general(place, low, dims, preferred_element_type=f32)
            put("f", 2 * which + c, moved)
    start("f")
    r_re, r_im, packed = denominators(me)

    arrive("ug")
    u = cat([get("ug", 0), get("ug", 1)], 1)
    g2 = cat([get("ug", 2), get("ug", 3)], 1)
    g1 = columns_derivative(u, t)
    g1_ref[...] = g1
    g2_ref[...] = g2
    pushed = u + (-0.5 * step) * (g1 * g1 + g2 * g2)
    arrive("t")
    goal = cat([get("t", 0), get("t", 1)], 1)
    for g, blocks in enumerate(columns_spectrum(cat([pushed, goal], 1), t)):
        for h in range(2):
            flat(send["wt"])[pl.ds(4 * h + g, 64, 8), :] = blocks[h]
    start("wt")

    arrive("f")
    own = (get("f", 0), get("f", 1))
    mirror = tuple(jnp.where(me == 0, roll(get("f", 2 + c), 16), get("f", 2 + c)) for c in range(2))
    here, there = waves_back([own, mirror], t)
    lane = lax.broadcasted_iota(jnp.int32, (128, 128), 1)
    column = lane % 64 // 8
    special = (column == 0) & (me == 0)
    for g in range(2):
        a = here[:, 128 * g : 128 * g + 128]
        b = there[:, 128 * g : 128 * g + 128]
        even = 0.5 * jnp.where(lane < 64, a + b, a - b)
        single = jnp.where(lane < 64, a, roll(b, 64))
        forced_ref[:, 128 * g : 128 * g + 128] = step * jnp.where(special, single, even)

    arrive("wt")
    w = cat([get("wt", 0), get("wt", 1)], 1) + forced_ref[...]
    goal = cat([get("wt", 2), get("wt", 3)], 1)
    z_re, z_im, t_re, t_im = waves_forward(cat([w, goal], 0), t)
    next_re = tuple(r_re * z for z in z_re)
    next_im = tuple(r_im * z for z in z_im)
    miss_re = tuple(a - b for a, b in zip(next_re, t_re))
    miss_im = tuple(a - b for a, b in zip(next_im, t_im))
    c_re = tuple((step * r_re) * v for v in miss_re)
    c_im = tuple((step * r_im) * v for v in miss_im)
    join = lambda x, y: (x[0] - y[1], x[1] + y[0])
    part = lambda x, y: (x[0] + y[1], x[1] - y[0])
    coef = join(c_re, c_im)
    m_out, n_out = waves_back([coef, join(next_re, next_im)], t)
    for g in range(2):
        put("m", g, m_out[:, 128 * g : 128 * g + 128])
    start("m")
    for g in range(2):
        put("n", g, n_out[:, 128 * g : 128 * g + 128])
    start("n")
    other = part(c_re, c_im)
    for c in range(2):
        put("fg", c, jnp.where(packed, c_re[c], coef[c]))
        back = jnp.where(packed, c_im[c], other[c])
        put("fg", 2 + c, jnp.where(me == 0, roll(back, 112), back))
    start("fg")
    miss = join(miss_re, miss_im)
    total = jnp.where(packed, 1.0, 2.0) * (miss[0] * miss[0] + miss[1] * miss[1])
    part_ref[...] = jnp.sum(total, axis=0, keepdims=True)
    parts_index = len(KEYS)
    parts_ref[me] = part_ref[...]

    def tell(j, carry):
        d = jnp.bitwise_xor(me, peers - j)
        pltpu.make_async_remote_copy(
            part_ref, parts_ref.at[me], send_sem.at[parts_index], recv_sem.at[parts_index],
            device_id=(d // 8, d % 8), device_id_type=MESH,
        ).start()
        return carry

    lax.fori_loop(1, peers, tell, 0)

    def blocks_of(key):
        return [
            tuple(get(key, 2 * h + g, 64, 4) for h in range(2))
            for g in range(2)
        ]

    arrive("m")
    m = columns_field(blocks_of("m"), t)
    q2 = m * g2_ref[...]
    for g in range(2):
        put("q", g, q2[:, 128 * g : 128 * g + 128])
    start("q")
    v = 4.0 * m + columns_derivative(m * g1_ref[...], t)
    for g in range(2):
        put("v", g, v[:, 128 * g : 128 * g + 128])
    start("v")
    arrive("n")
    stepped = columns_field(blocks_of("n"), t)
    for g in range(2):
        put("nx", g, stepped[:, 128 * g : 128 * g + 128])
    start("nx")

    arrive("fg")
    sides = []
    for which in range(2):
        block = cat([get("fg", 2 * which), get("fg", 2 * which + 1)], 1)
        high, low = split(block)
        place = t["places_t"][which]
        sides.append(dot(place, high) + dot(place, low))
    for h in range(2):
        for c in range(2):
            a = sides[0][128 * h : 128 * h + 128, 128 * c : 128 * c + 128].T
            b = sides[1][128 * h : 128 * h + 128, 128 * c : 128 * c + 128].T
            for k in range(8):
                at = 128 * (8 * h + k)
                fgrad_ref[c, :, at : at + 128] = (
                    a[16 * k : 16 * k + 16] + b[16 * (7 - k) : 16 * (7 - k) + 16]
                )
    pltpu.make_async_remote_copy(
        parts_ref.at[pl.ds(0, peers - 1)], parts_ref.at[pl.ds(0, peers - 1)],
        send_sem.at[parts_index], recv_sem.at[parts_index],
        device_id=(0, 0), device_id_type=MESH,
    ).wait_recv()
    sums = jnp.sum(flat(parts_ref)[...], axis=0, keepdims=True)
    objective_ref[...] = (0.5 / (n * n)) * jnp.sum(sums, axis=1, keepdims=True)
    arrive("q")
    slope = rows_derivative(get_tiles("q"), t)
    arrive("v")
    for i, tile in enumerate(get_tiles("v")):
        grad_ref[:, 128 * i : 128 * i + 128] = tile + slope[i]
    arrive("nx")
    for i, tile in enumerate(get_tiles("nx")):
        next_ref[:, 128 * i : 128 * i + 128] = tile
    for key in KEYS:
        whole(key).wait_send()
    pltpu.make_async_remote_copy(
        parts_ref.at[pl.ds(0, peers - 1)], parts_ref.at[pl.ds(0, peers - 1)],
        send_sem.at[parts_index], recv_sem.at[parts_index],
        device_id=(0, 0), device_id_type=MESH,
    ).wait_send()


def per_device(initial_field, target_field, forcing):
    built = build_tables()
    constants = [jnp.asarray(built[name]) for name in NAMES]
    vmem = pl.BlockSpec(memory_space=pltpu.VMEM)
    anywhere = pl.BlockSpec(memory_space=pl.ANY)
    messages = [pltpu.VMEM((peers, ROWS[key], 128), f32) for key in KEYS]
    next_field, objective, field_grad, forcing_grad = pl.pallas_call(
        kernel,
        out_shape=(
            jax.ShapeDtypeStruct((16, n), f32),
            jax.ShapeDtypeStruct((1, 1), f32),
            jax.ShapeDtypeStruct((16, n), f32),
            jax.ShapeDtypeStruct((2, 16, n), f32),
        ),
        in_specs=[vmem] * 3 + [anywhere] * len(NAMES),
        out_specs=(vmem,) * 4,
        scratch_shapes=[pltpu.VMEM(c.shape, c.dtype) for c in constants]
        + messages
        + messages
        + [
            pltpu.VMEM((1, 128), f32),
            pltpu.VMEM((peers, 1, 128), f32),
            pltpu.VMEM((128, 256), f32),
            pltpu.VMEM((128, 256), f32),
            pltpu.VMEM((128, 256), f32),
            pltpu.SemaphoreType.DMA((len(NAMES),)),
            pltpu.SemaphoreType.DMA((len(KEYS) + 1,)),
            pltpu.SemaphoreType.DMA((len(KEYS) + 1,)),
            pltpu.SemaphoreType.DMA((len(KEYS),)),
        ],
        compiler_params=pltpu.CompilerParams(
            collective_id=0, has_side_effects=True, vmem_limit_bytes=48 * 1024 * 1024
        ),
    )(initial_field[0], target_field[0], forcing, *constants)
    return next_field[None], objective.reshape(()), field_grad[None], forcing_grad


def solution(mesh):
    spec = P(None, ("px", "py"), None)
    return jax.shard_map(
        per_device,
        mesh=mesh,
        in_specs=(spec, spec, spec),
        out_specs=(spec, P(), spec, spec),
        check_vma=False,
    )
```

time: 373 us -> 69.1 us (0.19); the launches traced: 366 us -> 68.6 us
  waiting for transfers between devices: 110 us -> 0 us
  starting transfers between devices: 78.2 us -> 0 us
  local copies, waits for them, and re-layouts: 67.6 us -> 12.5 us
  matrix products: 54.7 us -> 0 us
  Pallas kernels: 0 us -> 53.7 us
  blocking collectives: 31.4 us -> 0 us
  other arithmetic: 18.9 us -> 0 us
    all_to_all x16 -> x0, waiting for transfers between devices: 110 us -> none  [one_exchange(): tiles = lax.all_to_all(tiles, axis, split_axis=0, concat_axis=0, tiled=True)]
    all_to_all x16 -> x0, starting transfers between devices: 78.2 us -> none  [one_exchange(): tiles = lax.all_to_all(tiles, axis, split_axis=0, concat_axis=0, tiled=True)]
    dot_general x116 -> x0, matrix products: 54.7 us -> none  [the longest x29 13.6 us: complex_einsum(): imag_term = jnp.einsum(formula, left_real, table_pair[1], precision=highest)]
    pallas_call x0 -> x1, Pallas kernels: none -> 53.7 us  [per_device(): pl.pallas_call(kernel, out_shape=(jax.ShapeDtypeStruct((16, n), f32), jax...]
    psum x4 -> x0, blocking collectives: 31.4 us -> none  [one_axis_at_a_time(): shard = lax.psum(shard, axis)]
    reshape x47 -> x0, local copies, waits for them, and re-layouts: 24.7 us -> none  [the longest x16 14.1 us: one_exchange(): tiles = laid_out(tiles.reshape(*sizes, *inside), concats[0] + 1)]
    all_to_all x16 -> x0, other arithmetic: 16.8 us -> none  [one_exchange(): tiles = lax.all_to_all(tiles, axis, split_axis=0, concat_axis=0, tiled=True)]
    unnamed x46 -> x25, local copies, waits for them, and re-layouts: 24.8 us -> 12.5 us
  transfers between devices with their start and end apart: 16 -> 0, of which waited for: 16 -> 0; matrix products, arithmetic and copies ran while one was open for 13% -> 0% of each run, Pallas kernels for 0% -> 0%
where the time goes in v2:
time: 69.1 us; the launch traced here: 68.6 us
  Pallas kernels  53.7 us (78%)
  local copies, waits for them, and re-layouts  12.5 us (18%)
  between operations  2.41 us (3%)
    pallas_call x1, Pallas kernels, per_device(): pl.pallas_call(kernel, out_shape=(jax.ShapeDtypeStruct((16, n), f32), jax...  53.7 us
    unnamed x25, local copies, waits for them, and re-layouts  12.5 us

profile of v2, /device:TPU:1, one launch (start us, length us, event | category | flops | bytes accessed | tf_op | source)
XLA Modules:
  0.0 68.6 jit_solution(13914091166223368274)
XLA Ops:
  0.6 0.0 copy-start
  0.6 1.7 %copy-done = bf16[9,2,256,256]{3,2,1,0:T(8,128)(2,1)S(1)} copy-done((bf16[9,2,256,256]{3,2,1,0:T(8,128)(2,1)S(1)}, bf16[9,2,256,256]{3,2,1,0:T(8,128)(2,1)}, u32[]{:S(2)}) %copy-start) | copy-done | bytes 2359320
  2.3 0.0 copy-start.1
  2.3 0.9 %copy-done.1 = f32[2,16,2048]{2,1,0:T(8,128)S(1)} copy-done((f32[2,16,2048]{2,1,0:T(8,128)S(1)}, f32[2,16,2048]{2,1,0:T(8,128)}, u32[]{:S(2)}) %copy-start.1) | copy-done | bytes 262168
  3.2 0.0 copy-start.2
  3.3 0.9 %copy-done.2 = f32[1,16,2048]{2,1,0:T(8,128)S(1)} copy-done((f32[1,16,2048]{2,1,0:T(8,128)S(1)}, f32[1,16,2048]{2,1,0:T(8,128)}, u32[]{:S(2)}) %copy-start.2) | copy-done | bytes 131096
  4.2 0.0 copy-start.3
  4.2 0.9 %copy-done.3 = f32[1,16,2048]{2,1,0:T(8,128)S(1)} copy-done((f32[1,16,2048]{2,1,0:T(8,128)S(1)}, f32[1,16,2048]{2,1,0:T(8,128)}, u32[]{:S(2)}) %copy-start.3) | copy-done | bytes 131096
  5.1 0.0 copy-start.4
  5.1 0.9 %copy-done.4 = f32[2,128,128]{2,1,0:T(8,128)S(1)} copy-done((f32[2,128,128]{2,1,0:T(8,128)S(1)}, f32[2,128,128]{2,1,0:T(8,128)}, u32[]{:S(2)}) %copy-start.4) | copy-done | bytes 131096
  6.0 0.0 copy-start.5
  6.0 0.9 %copy-done.5 = bf16[2,256,128]{2,1,0:T(8,128)(2,1)S(1)} copy-done((bf16[2,256,128]{2,1,0:T(8,128)(2,1)S(1)}, bf16[2,256,128]{2,1,0:T(8,128)(2,1)}, u32[]{:S(2)}) %copy-start.5) | copy-done | bytes 131096
  6.9 0.9 %copy-done.6 = bf16[2,128,256]{2,1,0:T(8,128)(2,1)S(1)} copy-done((bf16[2,128,256]{2,1,0:T(8,128)(2,1)S(1)}, bf16[2,128,256]{2,1,0:T(8,128)(2,1)}, u32[]{:S(2)}) %copy-start.6) | copy-done | bytes 131096
  7.8 0.0 copy-start.7
  7.8 0.9 %copy-done.7 = bf16[2,128,144]{2,1,0:T(8,128)(2,1)S(1)} copy-done((bf16[2,128,144]{2,1,0:T(8,128)(2,1)S(1)}, bf16[2,128,144]{2,1,0:T(8,128)(2,1)}, u32[]{:S(2)}) %copy-start.7) | copy-done | bytes 73752
  8.7 0.0 copy-start.8
  8.7 0.9 %copy-done.8 = f32[2,72,128]{2,1,0:T(8,128)S(1)} copy-done((f32[2,72,128]{2,1,0:T(8,128)S(1)}, f32[2,72,128]{2,1,0:T(8,128)}, u32[]{:S(2)}) %copy-start.8) | copy-done | bytes 73752
  9.6 0.0 copy-start.9
  9.6 0.9 %copy-done.9 = bf16[2,144,128]{2,1,0:T(8,128)(2,1)S(1)} copy-done((bf16[2,144,128]{2,1,0:T(8,128)(2,1)S(1)}, bf16[2,144,128]{2,1,0:T(8,128)(2,1)}, u32[]{:S(2)}) %copy-start.9) | copy-done | bytes 73752
  10.4 0.7 %copy-done.10 = f32[2,16,128]{2,1,0:T(8,128)S(1)} copy-done((f32[2,16,128]{2,1,0:T(8,128)S(1)}, f32[2,16,128]{2,1,0:T(8,128)}, u32[]{:S(2)}) %copy-start.10) | copy-done | bytes 16408
  11.2 53.7 %shard_map.138 = (f32[16,2048]{1,0:T(8,128)S(1)}, f32[1,1]{1,0:T(1,128)}, f32[16,2048]{1,0:T(8,128)S(1)}, f32[2,16,2048]{2,1,0:T(8,128)S(1)}) custom-call(f32[16,2048]{1,0:T(8,128)S(1)} %bitcast.5, f32[16,2048]{1,0:T(8,128)S(1)} %bitcast.6, f32[2,16,2048]{2,1,0:T(8,128)S(1)} %copy-done.1, bf16[9,2,256,256]{3,2,1,0:T(8,128)(2,1)S(1)} %copy-done, ...), custom_call_target="tpu_custom_call" | custom-call | tf_op jit(solution)/shard_map/pallas_call | solution.py:618
  64.9 0.7 copy.19
  66.1 0.7 copy.21
  66.8 0.7 %copy.22 = f32[2,16,2048]{2,1,0:T(8,128)} copy(f32[2,16,2048]{2,1,0:T(8,128)S(1)} %get-tuple-element.19) | data formatting | bytes 524288
  (2 shorter events, 0.0 us)
Async XLA Ops:
  0.6 1.7 %copy-start = (bf16[9,2,256,256]{3,2,1,0:T(8,128)(2,1)S(1)}, bf16[9,2,256,256]{3,2,1,0:T(8,128)(2,1)}, u32[]{:S(2)}) copy-start(bf16[9,2,256,256]{3,2,1,0:T(8,128)(2,1)} %constant.16.clone.refs_3_) | copy-start | bytes 7077892
  2.3 0.9 %copy-start.1 = (f32[2,16,2048]{2,1,0:T(8,128)S(1)}, f32[2,16,2048]{2,1,0:T(8,128)}, u32[]{:S(2)}) copy-start(f32[2,16,2048]{2,1,0:T(8,128)} %refs_2_.1) | copy-start | bytes 786436
  3.2 0.9 %copy-start.2 = (f32[1,16,2048]{2,1,0:T(8,128)S(1)}, f32[1,16,2048]{2,1,0:T(8,128)}, u32[]{:S(2)}) copy-start(f32[1,16,2048]{2,1,0:T(8,128)} %param.11) | copy-start | bytes 393220
  4.2 0.9 %copy-start.3 = (f32[1,16,2048]{2,1,0:T(8,128)S(1)}, f32[1,16,2048]{2,1,0:T(8,128)}, u32[]{:S(2)}) copy-start(f32[1,16,2048]{2,1,0:T(8,128)} %param.12) | copy-start | bytes 393220
  5.1 0.9 %copy-start.4 = (f32[2,128,128]{2,1,0:T(8,128)S(1)}, f32[2,128,128]{2,1,0:T(8,128)}, u32[]{:S(2)}) copy-start(f32[2,128,128]{2,1,0:T(8,128)} %constant.22.clone.refs_9_) | copy-start | bytes 393220
  6.0 0.9 %copy-start.5 = (bf16[2,256,128]{2,1,0:T(8,128)(2,1)S(1)}, bf16[2,256,128]{2,1,0:T(8,128)(2,1)}, u32[]{:S(2)}) copy-start(bf16[2,256,128]{2,1,0:T(8,128)(2,1)} %constant.20.clone.refs_7_) | copy-start | bytes 393220
  6.9 0.9 %copy-start.6 = (bf16[2,128,256]{2,1,0:T(8,128)(2,1)S(1)}, bf16[2,128,256]{2,1,0:T(8,128)(2,1)}, u32[]{:S(2)}) copy-start(bf16[2,128,256]{2,1,0:T(8,128)(2,1)} %constant.19.clone.refs_6_) | copy-start | bytes 393220
  7.8 0.9 %copy-start.7 = (bf16[2,128,144]{2,1,0:T(8,128)(2,1)S(1)}, bf16[2,128,144]{2,1,0:T(8,128)(2,1)}, u32[]{:S(2)}) copy-start(bf16[2,128,144]{2,1,0:T(8,128)(2,1)} %constant.18.clone.refs_5_) | copy-start | bytes 221188
  8.7 0.9 %copy-start.8 = (f32[2,72,128]{2,1,0:T(8,128)S(1)}, f32[2,72,128]{2,1,0:T(8,128)}, u32[]{:S(2)}) copy-start(f32[2,72,128]{2,1,0:T(8,128)} %constant.21.clone.refs_8_) | copy-start | bytes 221188
  9.6 0.9 %copy-start.9 = (bf16[2,144,128]{2,1,0:T(8,128)(2,1)S(1)}, bf16[2,144,128]{2,1,0:T(8,128)(2,1)}, u32[]{:S(2)}) copy-start(bf16[2,144,128]{2,1,0:T(8,128)(2,1)} %constant.17.clone.refs_4_) | copy-start | bytes 221188
  10.4 0.7 %copy-start.10 = (f32[2,16,128]{2,1,0:T(8,128)S(1)}, f32[2,16,128]{2,1,0:T(8,128)}, u32[]{:S(2)}) copy-start(f32[2,16,128]{2,1,0:T(8,128)} %constant.23.clone.refs_10_) | copy-start | bytes 49156

commit v3 on v2

--- a/solution.py
+++ b/solution.py
@@ -8,7 +8,7 @@
 from jax.experimental.pallas import tpu as pltpu
 from jax.sharding import PartitionSpec as P
 
-MESH = pl.DeviceIdType.MESH
+LOGICAL = pl.DeviceIdType.LOGICAL
 f32 = jnp.float32
 bf16 = jnp.bfloat16
 
@@ -368,18 +368,24 @@
 KEYS = tuple(ROWS)
 
 
+RECEIVED = tuple(key for key in KEYS if key not in ("v", "nx"))
+
+
 def kernel(*refs):
-    u_ref, t_ref, f_ref = refs[:3]
+    fields_hbm = refs[:3]
     tables_hbm = refs[3 : 3 + len(NAMES)]
     refs = refs[3 + len(NAMES) :]
-    next_ref, objective_ref, grad_ref, fgrad_ref = refs[:4]
-    refs = refs[4:]
+    objective_ref, slope_ref, fgrad_ref = refs[:3]
+    recv = dict(zip(("v", "nx"), refs[3:5]))
+    refs = refs[5:]
+    u_ref, t_ref, f_ref = refs[:3]
+    refs = refs[3:]
     tables = dict(zip(NAMES, refs[: len(NAMES)]))
     refs = refs[len(NAMES) :]
     send = dict(zip(KEYS, refs[: len(KEYS)]))
     refs = refs[len(KEYS) :]
-    recv = dict(zip(KEYS, refs[: len(KEYS)]))
-    refs = refs[len(KEYS) :]
+    recv.update(zip(RECEIVED, refs[: len(RECEIVED)]))
+    refs = refs[len(RECEIVED) :]
     part_ref, parts_ref, g1_ref, g2_ref, forced_ref = refs[:5]
     table_sem, send_sem, recv_sem, own_sem = refs[5:]
 
@@ -387,17 +393,19 @@
     barrier = pltpu.get_barrier_semaphore()
 
     def greet(i, carry):
-        d = jnp.bitwise_xor(me, i)
-        pl.semaphore_signal(barrier, inc=1, device_id=(d // 8, d % 8), device_id_type=MESH)
+        d = jnp.bitwise_xor(me, peers - i)
+        pl.semaphore_signal(barrier, inc=1, device_id=d, device_id_type=LOGICAL)
         return carry
 
+    lax.fori_loop(1, peers, greet, 0, unroll=4)
     loads = [
-        pltpu.make_async_copy(src, tables[name], table_sem.at[i])
-        for i, (name, src) in enumerate(zip(NAMES, tables_hbm))
+        pltpu.make_async_copy(src, dst, table_sem.at[i])
+        for i, (src, dst) in enumerate(
+            zip(fields_hbm + tables_hbm, [u_ref, t_ref, f_ref] + [tables[k] for k in NAMES])
+        )
     ]
     for load in loads:
         load.start()
-    lax.fori_loop(1, peers, greet, 0)
 
     def flat(ref):
         return ref.reshape(ref.shape[0] * ref.shape[1], 128)
@@ -417,18 +425,18 @@
             d = jnp.bitwise_xor(me, peers - j)
             pltpu.make_async_remote_copy(
                 src.at[d], dst.at[me], send_sem.at[i], recv_sem.at[i],
-                device_id=(d // 8, d % 8), device_id_type=MESH,
+                device_id=d, device_id_type=LOGICAL,
             ).start()
             return carry
 
-        lax.fori_loop(1, peers, one, 0)
+        lax.fori_loop(1, peers, one, 0, unroll=4)
 
     def whole(key):
         i = KEYS.index(key)
         span = pl.ds(0, peers - 1)
         return pltpu.make_async_remote_copy(
             send[key].at[span], recv[key].at[span], send_sem.at[i], recv_sem.at[i],
-            device_id=(0, 0), device_id_type=MESH,
+            device_id=0, device_id_type=LOGICAL,
         )
 
     def arrive(key):
@@ -541,11 +549,11 @@
         d = jnp.bitwise_xor(me, peers - j)
         pltpu.make_async_remote_copy(
             part_ref, parts_ref.at[me], send_sem.at[parts_index], recv_sem.at[parts_index],
-            device_id=(d // 8, d % 8), device_id_type=MESH,
+            device_id=d, device_id_type=LOGICAL,
         ).start()
         return carry
 
-    lax.fori_loop(1, peers, tell, 0)
+    lax.fori_loop(1, peers, tell, 0, unroll=4)
 
     def blocks_of(key):
         return [
@@ -588,61 +596,98 @@
     pltpu.make_async_remote_copy(
         parts_ref.at[pl.ds(0, peers - 1)], parts_ref.at[pl.ds(0, peers - 1)],
         send_sem.at[parts_index], recv_sem.at[parts_index],
-        device_id=(0, 0), device_id_type=MESH,
+        device_id=0, device_id_type=LOGICAL,
     ).wait_recv()
     sums = jnp.sum(flat(parts_ref)[...], axis=0, keepdims=True)
     objective_ref[...] = (0.5 / (n * n)) * jnp.sum(sums, axis=1, keepdims=True)
     arrive("q")
-    slope = rows_derivative(get_tiles("q"), t)
+    for i, tile in enumerate(rows_derivative(get_tiles("q"), t)):
+        slope_ref[:, 128 * i : 128 * i + 128] = tile
     arrive("v")
-    for i, tile in enumerate(get_tiles("v")):
-        grad_ref[:, 128 * i : 128 * i + 128] = tile + slope[i]
     arrive("nx")
-    for i, tile in enumerate(get_tiles("nx")):
-        next_ref[:, 128 * i : 128 * i + 128] = tile
     for key in KEYS:
         whole(key).wait_send()
     pltpu.make_async_remote_copy(
         parts_ref.at[pl.ds(0, peers - 1)], parts_ref.at[pl.ds(0, peers - 1)],
         send_sem.at[parts_index], recv_sem.at[parts_index],
-        device_id=(0, 0), device_id_type=MESH,
+        device_id=0, device_id_type=LOGICAL,
     ).wait_send()
+
+
+def finish(
+    total_ref, slope_ref, fgrad_ref, v_ref, nx_ref,
+    objective_out, grad_out, next_out, fgrad_out, grad, nexts, sems,
+):
+    objective_out[...] = total_ref[...]
+    copies = [
+        pltpu.make_async_copy(src, dst, sems.at[i])
+        for i, (src, dst) in enumerate(
+            ((fgrad_ref, fgrad_out), (grad, grad_out), (nexts, next_out))
+        )
+    ]
+    copies[0].start()
+    for ref, out, i in ((v_ref, grad, 1), (nx_ref, nexts, 2)):
+        for g in range(2):
+            block = ref.reshape(2 * peers, 128)[pl.ds(g, peers, 2), :].T
+            for k in range(8):
+                at = 128 * (8 * g + k)
+                tile = block[16 * k : 16 * k + 16]
+                if i == 1:
+                    tile = tile + slope_ref[:, at : at + 128]
+                out[:, at : at + 128] = tile
+        copies[i].start()
+    for copy in copies:
+        copy.wait()
 
 
 def per_device(initial_field, target_field, forcing):
     built = build_tables()
     constants = [jnp.asarray(built[name]) for name in NAMES]
     vmem = pl.BlockSpec(memory_space=pltpu.VMEM)
-    anywhere = pl.BlockSpec(memory_space=pl.ANY)
-    messages = [pltpu.VMEM((peers, ROWS[key], 128), f32) for key in KEYS]
-    next_field, objective, field_grad, forcing_grad = pl.pallas_call(
+    hbm = pl.BlockSpec(memory_space=pltpu.HBM)
+    message = lambda key: pltpu.VMEM((peers, ROWS[key], 128), f32)
+    operands = tuple(
+        pltpu.with_memory_space_constraint(x, pltpu.HBM)
+        for x in (initial_field[0], target_field[0], forcing, *constants)
+    )
+    field = jax.ShapeDtypeStruct((16, n), f32)
+    both = jax.ShapeDtypeStruct((2, 16, n), f32)
+    landing = jax.ShapeDtypeStruct((peers, 2, 128), f32)
+    total, slope, forcing_rows, v, nx = pl.pallas_call(
         kernel,
-        out_shape=(
-            jax.ShapeDtypeStruct((16, n), f32),
-            jax.ShapeDtypeStruct((1, 1), f32),
-            jax.ShapeDtypeStruct((16, n), f32),
-            jax.ShapeDtypeStruct((2, 16, n), f32),
-        ),
-        in_specs=[vmem] * 3 + [anywhere] * len(NAMES),
-        out_specs=(vmem,) * 4,
-        scratch_shapes=[pltpu.VMEM(c.shape, c.dtype) for c in constants]
-        + messages
-        + messages
+        out_shape=(jax.ShapeDtypeStruct((1, 1), f32), field, both, landing, landing),
+        in_specs=[hbm] * len(operands),
+        out_specs=(vmem,) * 5,
+        scratch_shapes=[pltpu.VMEM(x.shape, x.dtype) for x in operands]
+        + [message(key) for key in KEYS]
+        + [message(key) for key in RECEIVED]
         + [
             pltpu.VMEM((1, 128), f32),
             pltpu.VMEM((peers, 1, 128), f32),
             pltpu.VMEM((128, 256), f32),
             pltpu.VMEM((128, 256), f32),
             pltpu.VMEM((128, 256), f32),
-            pltpu.SemaphoreType.DMA((len(NAMES),)),
+            pltpu.SemaphoreType.DMA((len(operands),)),
             pltpu.SemaphoreType.DMA((len(KEYS) + 1,)),
             pltpu.SemaphoreType.DMA((len(KEYS) + 1,)),
             pltpu.SemaphoreType.DMA((len(KEYS),)),
         ],
         compiler_params=pltpu.CompilerParams(
-            collective_id=0, has_side_effects=True, vmem_limit_bytes=48 * 1024 * 1024
+            collective_id=0, has_side_effects=True, vmem_limit_bytes=32 * 1024 * 1024
         ),
-    )(initial_field[0], target_field[0], forcing, *constants)
+    )(*operands)
+    objective, field_grad, next_field, forcing_grad = pl.pallas_call(
+        finish,
+        out_shape=(jax.ShapeDtypeStruct((1, 1), f32), field, field, both),
+        in_specs=[vmem] * 5,
+        out_specs=(vmem,) + (hbm,) * 3,
+        scratch_shapes=[
+            pltpu.VMEM((16, n), f32),
+            pltpu.VMEM((16, n), f32),
+            pltpu.SemaphoreType.DMA((3,)),
+        ],
+        compiler_params=pltpu.CompilerParams(vmem_limit_bytes=8 * 1024 * 1024),
+    )(total, slope, forcing_rows, v, nx)
     return next_field[None], objective.reshape(()), field_grad[None], forcing_grad
 
 

time: 69.1 us -> 48.7 us (0.70)
  local copies, waits for them, and re-layouts: 12.5 us -> 0 us
  Pallas kernels: 53.7 us -> 47.9 us
  between operations: 2.41 us -> 0.64 us
    unnamed x25 -> x0, local copies, waits for them, and re-layouts: 12.5 us -> none
    pallas_call x1 -> x2, Pallas kernels: 53.7 us -> 47.9 us  [the longest x1 45.9 us: per_device(): pl.pallas_call(kernel, out_shape=(jax.ShapeDtypeStruct((1, 1), f32), fiel...]
where the time goes in v3:
time: 48.7 us; the launch traced here: 48.5 us
  Pallas kernels  47.9 us (98%)
  between operations  0.64 us (1%)
    pallas_call x1, Pallas kernels, per_device(): pl.pallas_call(kernel, out_shape=(jax.ShapeDtypeStruct((1, 1), f32), fiel...  45.9 us
    pallas_call x1, Pallas kernels, per_device(): pl.pallas_call(finish, out_shape=(jax.ShapeDtypeStruct((1, 1), f32), fiel...  1.98 us

profile of v3, /device:TPU:1, one launch (start us, length us, event | category | flops | bytes accessed | tf_op | source)
XLA Modules:
  0.0 48.5 jit_solution(2797326278378739131)
XLA Ops:
  0.6 45.9 %shard_map.138 = (f32[1,1]{1,0:T(1,128)}, f32[16,2048]{1,0:T(8,128)S(1)}, f32[2,16,2048]{2,1,0:T(8,128)S(1)}, f32[128,2,128]{2,1,0:T(2,128)S(1)}, f32[128,2,128]{2,1,0:T(2,128)S(1)}) custom-call(f32[16,2048]{1,0:T(8,128)} %bitcast.5, f32[16,2048]{1,0:T(8,128)} %bitcast.6, f32[2,16,2048]{2,1,0:T(8,128)} %refs_2_.1, ...), custom_call_target="tpu_custom_call" | custom-call | tf_op jit(solution)/shard_map/pallas_call | solution.py:656
  46.5 2.0 %shard_map.139 = (f32[1,1]{1,0:T(1,128)}, f32[16,2048]{1,0:T(8,128)}, f32[16,2048]{1,0:T(8,128)}, f32[2,16,2048]{2,1,0:T(8,128)}) custom-call(f32[1,1]{1,0:T(1,128)} %get-tuple-element.13.total_ref, f32[16,2048]{1,0:T(8,128)S(1)} %get-tuple-element.14.slope_ref, f32[2,16,2048]{2,1,0:T(8,128)S(1)} %get-tuple-element.15.fgrad_ref, ...), custom_call_target="tpu_custom_call" | custom-call | tf_op jit(solution)/shard_map/pallas_call | solution.py:679

commit v4 on v3

--- a/solution.py
+++ b/solution.py
@@ -364,11 +364,19 @@
     return out[0], out[1], packed
 
 
-ROWS = dict(ug=4, t=2, f=4, wt=4, m=2, n=2, fg=4, q=2, v=2, nx=2)
+ROWS = dict(t=2, ug=4, f=4, goal=2, w=2, m=2, n=2, fg=4, qv=4, nx=2)
 KEYS = tuple(ROWS)
-
-
-RECEIVED = tuple(key for key in KEYS if key not in ("v", "nx"))
+DIRECT = ("ug", "w", "m", "qv", "f")
+
+
+def hops(offset):
+    return sum((0, 1, 2, 1)[offset >> shift & 3] for shift in (1, 3, 5))
+
+
+FAR_FIRST = sorted(range(peers - 1, 0, -1), key=lambda offset: -hops(offset))
+
+
+RECEIVED = tuple(key for key in KEYS if key not in ("qv", "nx"))
 
 
 def kernel(*refs):
@@ -376,7 +384,7 @@
     tables_hbm = refs[3 : 3 + len(NAMES)]
     refs = refs[3 + len(NAMES) :]
     objective_ref, slope_ref, fgrad_ref = refs[:3]
-    recv = dict(zip(("v", "nx"), refs[3:5]))
+    recv = dict(zip(("qv", "nx"), refs[3:5]))
     refs = refs[5:]
     u_ref, t_ref, f_ref = refs[:3]
     refs = refs[3:]
@@ -386,8 +394,8 @@
     refs = refs[len(KEYS) :]
     recv.update(zip(RECEIVED, refs[: len(RECEIVED)]))
     refs = refs[len(RECEIVED) :]
-    part_ref, parts_ref, g1_ref, g2_ref, forced_ref = refs[:5]
-    table_sem, send_sem, recv_sem, own_sem = refs[5:]
+    part_ref, mid_ref, near_ref, far_ref, g1_ref, g2_ref, forced_ref, goal_ref = refs[:8]
+    table_sem, send_sem, recv_sem, own_sem = refs[8:]
 
     me = lax.axis_index("px") * 8 + lax.axis_index("py")
     barrier = pltpu.get_barrier_semaphore()
@@ -421,15 +429,18 @@
         src, dst = send[key], recv[key]
         pltpu.make_async_copy(src.at[me], dst.at[me], own_sem.at[i]).start()
 
-        def one(j, carry):
-            d = jnp.bitwise_xor(me, peers - j)
+        def one(offset):
+            d = jnp.bitwise_xor(me, offset)
             pltpu.make_async_remote_copy(
                 src.at[d], dst.at[me], send_sem.at[i], recv_sem.at[i],
                 device_id=d, device_id_type=LOGICAL,
             ).start()
-            return carry
-
-        lax.fori_loop(1, peers, one, 0, unroll=4)
+
+        if key in DIRECT:
+            for offset in FAR_FIRST:
+                one(offset)
+        else:
+            lax.fori_loop(1, peers, lambda j, c: (one(peers - j), c)[1], 0, unroll=4)
 
     def whole(key):
         i = KEYS.index(key)
@@ -444,6 +455,23 @@
         pltpu.make_async_copy(send[key].at[me], recv[key].at[me], own_sem.at[i]).wait()
         whole(key).wait_recv()
 
+    group, member = jnp.bitwise_and(me, 7), lax.shift_right_logical(me, 3)
+    near, far = len(KEYS), len(KEYS) + 1
+
+    def tell(src, dst, sem, offsets):
+        for offset in offsets:
+            pltpu.make_async_remote_copy(
+                src, dst, send_sem.at[sem], recv_sem.at[sem],
+                device_id=jnp.bitwise_xor(me, offset), device_id_type=LOGICAL,
+            ).start()
+
+    def told(ref, sem):
+        others = ref.at[pl.ds(0, ref.shape[0] - 1)]
+        return pltpu.make_async_remote_copy(
+            others, others, send_sem.at[sem], recv_sem.at[sem],
+            device_id=0, device_id_type=LOGICAL,
+        )
+
     def tiles_of(ref):
         return [ref[:, 128 * i : 128 * i + 128] for i in range(16)]
 
@@ -465,9 +493,6 @@
     put_field("ug", 0, u_tiles)
     put_field("ug", 2, rows_derivative(u_tiles, t))
     put_field("t", 0, tiles_of(t_ref))
-    pl.semaphore_wait(barrier, peers - 1)
-    start("ug")
-    start("t")
     for c in range(2):
         for which in range(2):
             sides = []
@@ -482,22 +507,28 @@
             moved = lax.dot_general(place, high, dims, preferred_element_type=f32)
             moved = moved + lax.dot_general(place, low, dims, preferred_element_type=f32)
             put("f", 2 * which + c, moved)
+    pl.semaphore_wait(barrier, peers - 1)
+    start("t")
+    start("ug")
     start("f")
     r_re, r_im, packed = denominators(me)
 
+    def put_spectrum(key, field):
+        for g, blocks in enumerate(columns_spectrum(field, t)):
+            for h in range(2):
+                flat(send[key])[pl.ds(2 * h + g, 64, 4), :] = blocks[h]
+
+    arrive("t")
+    put_spectrum("goal", cat([get("t", 0), get("t", 1)], 1))
+    start("goal")
     arrive("ug")
     u = cat([get("ug", 0), get("ug", 1)], 1)
     g2 = cat([get("ug", 2), get("ug", 3)], 1)
     g1 = columns_derivative(u, t)
     g1_ref[...] = g1
     g2_ref[...] = g2
-    pushed = u + (-0.5 * step) * (g1 * g1 + g2 * g2)
-    arrive("t")
-    goal = cat([get("t", 0), get("t", 1)], 1)
-    for g, blocks in enumerate(columns_spectrum(cat([pushed, goal], 1), t)):
-        for h in range(2):
-            flat(send["wt"])[pl.ds(4 * h + g, 64, 8), :] = blocks[h]
-    start("wt")
+    put_spectrum("w", u + (-0.5 * step) * (g1 * g1 + g2 * g2))
+    start("w")
 
     arrive("f")
     own = (get("f", 0), get("f", 1))
@@ -513,10 +544,14 @@
         single = jnp.where(lane < 64, a, roll(b, 64))
         forced_ref[:, 128 * g : 128 * g + 128] = step * jnp.where(special, single, even)
 
-    arrive("wt")
-    w = cat([get("wt", 0), get("wt", 1)], 1) + forced_ref[...]
-    goal = cat([get("wt", 2), get("wt", 3)], 1)
-    z_re, z_im, t_re, t_im = waves_forward(cat([w, goal], 0), t)
+    arrive("goal")
+    for i, (re, im) in enumerate(waves_forward(cat([get("goal", 0), get("goal", 1)], 1), t)):
+        goal_ref[2 * i] = re
+        goal_ref[2 * i + 1] = im
+    arrive("w")
+    w = cat([get("w", 0), get("w", 1)], 1) + forced_ref[...]
+    z_re, z_im = waves_forward(w, t)
+    t_re, t_im = (goal_ref[0], goal_ref[1]), (goal_ref[2], goal_ref[3])
     next_re = tuple(r_re * z for z in z_re)
     next_im = tuple(r_im * z for z in z_im)
     miss_re = tuple(a - b for a, b in zip(next_re, t_re))
@@ -526,10 +561,11 @@
     join = lambda x, y: (x[0] - y[1], x[1] + y[0])
     part = lambda x, y: (x[0] + y[1], x[1] - y[0])
     coef = join(c_re, c_im)
-    m_out, n_out = waves_back([coef, join(next_re, next_im)], t)
+    (m_out,) = waves_back([coef], t)
     for g in range(2):
         put("m", g, m_out[:, 128 * g : 128 * g + 128])
     start("m")
+    (n_out,) = waves_back([join(next_re, next_im)], t)
     for g in range(2):
         put("n", g, n_out[:, 128 * g : 128 * g + 128])
     start("n")
@@ -542,18 +578,8 @@
     miss = join(miss_re, miss_im)
     total = jnp.where(packed, 1.0, 2.0) * (miss[0] * miss[0] + miss[1] * miss[1])
     part_ref[...] = jnp.sum(total, axis=0, keepdims=True)
-    parts_index = len(KEYS)
-    parts_ref[me] = part_ref[...]
-
-    def tell(j, carry):
-        d = jnp.bitwise_xor(me, peers - j)
-        pltpu.make_async_remote_copy(
-            part_ref, parts_ref.at[me], send_sem.at[parts_index], recv_sem.at[parts_index],
-            device_id=d, device_id_type=LOGICAL,
-        ).start()
-        return carry
-
-    lax.fori_loop(1, peers, tell, 0, unroll=4)
+    near_ref[group] = part_ref[...]
+    tell(part_ref, near_ref.at[group], near, [j for j in range(1, 8)])
 
     def blocks_of(key):
         return [
@@ -564,13 +590,15 @@
     arrive("m")
     m = columns_field(blocks_of("m"), t)
     q2 = m * g2_ref[...]
-    for g in range(2):
-        put("q", g, q2[:, 128 * g : 128 * g + 128])
-    start("q")
     v = 4.0 * m + columns_derivative(m * g1_ref[...], t)
     for g in range(2):
-        put("v", g, v[:, 128 * g : 128 * g + 128])
-    start("v")
+        put("qv", g, q2[:, 128 * g : 128 * g + 128])
+        put("qv", 2 + g, v[:, 128 * g : 128 * g + 128])
+    start("qv")
+    told(near_ref, near).wait_recv()
+    mid_ref[...] = jnp.sum(flat(near_ref)[...], axis=0, keepdims=True)
+    far_ref[member] = mid_ref[...]
+    tell(mid_ref, far_ref.at[member], far, [8 * j for j in range(1, 16)])
     arrive("n")
     stepped = columns_field(blocks_of("n"), t)
     for g in range(2):
@@ -593,25 +621,17 @@
                 fgrad_ref[c, :, at : at + 128] = (
                     a[16 * k : 16 * k + 16] + b[16 * (7 - k) : 16 * (7 - k) + 16]
                 )
-    pltpu.make_async_remote_copy(
-        parts_ref.at[pl.ds(0, peers - 1)], parts_ref.at[pl.ds(0, peers - 1)],
-        send_sem.at[parts_index], recv_sem.at[parts_index],
-        device_id=0, device_id_type=LOGICAL,
-    ).wait_recv()
-    sums = jnp.sum(flat(parts_ref)[...], axis=0, keepdims=True)
+    told(far_ref, far).wait_recv()
+    sums = jnp.sum(flat(far_ref)[...], axis=0, keepdims=True)
     objective_ref[...] = (0.5 / (n * n)) * jnp.sum(sums, axis=1, keepdims=True)
-    arrive("q")
-    for i, tile in enumerate(rows_derivative(get_tiles("q"), t)):
+    arrive("qv")
+    for i, tile in enumerate(rows_derivative(get_tiles("qv"), t)):
         slope_ref[:, 128 * i : 128 * i + 128] = tile
-    arrive("v")
     arrive("nx")
     for key in KEYS:
         whole(key).wait_send()
-    pltpu.make_async_remote_copy(
-        parts_ref.at[pl.ds(0, peers - 1)], parts_ref.at[pl.ds(0, peers - 1)],
-        send_sem.at[parts_index], recv_sem.at[parts_index],
-        device_id=0, device_id_type=LOGICAL,
-    ).wait_send()
+    told(near_ref, near).wait_send()
+    told(far_ref, far).wait_send()
 
 
 def finish(
@@ -626,9 +646,9 @@
         )
     ]
     copies[0].start()
-    for ref, out, i in ((v_ref, grad, 1), (nx_ref, nexts, 2)):
+    for ref, out, i, rows, first in ((v_ref, grad, 1, 4, 2), (nx_ref, nexts, 2, 2, 0)):
         for g in range(2):
-            block = ref.reshape(2 * peers, 128)[pl.ds(g, peers, 2), :].T
+            block = ref.reshape(rows * peers, 128)[pl.ds(first + g, peers, rows), :].T
             for k in range(8):
                 at = 128 * (8 * g + k)
                 tile = block[16 * k : 16 * k + 16]
@@ -652,10 +672,10 @@
     )
     field = jax.ShapeDtypeStruct((16, n), f32)
     both = jax.ShapeDtypeStruct((2, 16, n), f32)
-    landing = jax.ShapeDtypeStruct((peers, 2, 128), f32)
+    landing = [jax.ShapeDtypeStruct((peers, ROWS[key], 128), f32) for key in ("qv", "nx")]
     total, slope, forcing_rows, v, nx = pl.pallas_call(
         kernel,
-        out_shape=(jax.ShapeDtypeStruct((1, 1), f32), field, both, landing, landing),
+        out_shape=(jax.ShapeDtypeStruct((1, 1), f32), field, both, *landing),
         in_specs=[hbm] * len(operands),
         out_specs=(vmem,) * 5,
         scratch_shapes=[pltpu.VMEM(x.shape, x.dtype) for x in operands]
@@ -663,13 +683,16 @@
         + [message(key) for key in RECEIVED]
         + [
             pltpu.VMEM((1, 128), f32),
-            pltpu.VMEM((peers, 1, 128), f32),
+            pltpu.VMEM((1, 128), f32),
+            pltpu.VMEM((8, 1, 128), f32),
+            pltpu.VMEM((16, 1, 128), f32),
             pltpu.VMEM((128, 256), f32),
             pltpu.VMEM((128, 256), f32),
             pltpu.VMEM((128, 256), f32),
+            pltpu.VMEM((4, 128, 128), f32),
             pltpu.SemaphoreType.DMA((len(operands),)),
-            pltpu.SemaphoreType.DMA((len(KEYS) + 1,)),
-            pltpu.SemaphoreType.DMA((len(KEYS) + 1,)),
+            pltpu.SemaphoreType.DMA((len(KEYS) + 2,)),
+            pltpu.SemaphoreType.DMA((len(KEYS) + 2,)),
             pltpu.SemaphoreType.DMA((len(KEYS),)),
         ],
         compiler_params=pltpu.CompilerParams(

time: 48.7 us -> 47.4 us (0.973)
  Pallas kernels: 47.9 us -> 46.6 us
    pallas_call x1, Pallas kernels: 45.9 us -> 44.7 us  [per_device(): pl.pallas_call(kernel, out_shape=(jax.ShapeDtypeStruct((1, 1), f32), fiel...]
where the time goes in v4:
time: 47.4 us; the launch traced here: 47.3 us
  Pallas kernels  46.6 us (98%)
  between operations  0.64 us (1%)
    pallas_call x1, Pallas kernels, per_device(): pl.pallas_call(kernel, out_shape=(jax.ShapeDtypeStruct((1, 1), f32), fiel...  44.7 us
    pallas_call x1, Pallas kernels, per_device(): pl.pallas_call(finish, out_shape=(jax.ShapeDtypeStruct((1, 1), f32), fiel...  1.97 us

profile of v4, /device:TPU:1, one launch (start us, length us, event | category | flops | bytes accessed | tf_op | source)
XLA Modules:
  0.0 47.3 jit_solution(5919578175073941257)
XLA Ops:
  0.6 44.7 %shard_map.138 = (f32[1,1]{1,0:T(1,128)}, f32[16,2048]{1,0:T(8,128)S(1)}, f32[2,16,2048]{2,1,0:T(8,128)S(1)}, f32[128,4,128]{2,1,0:T(4,128)S(1)}, f32[128,2,128]{2,1,0:T(2,128)S(1)}) custom-call(f32[16,2048]{1,0:T(8,128)} %bitcast.5, f32[16,2048]{1,0:T(8,128)} %bitcast.6, f32[2,16,2048]{2,1,0:T(8,128)} %refs_2_.1, ...), custom_call_target="tpu_custom_call" | custom-call | tf_op jit(solution)/shard_map/pallas_call | solution.py:676
  45.3 2.0 %shard_map.139 = (f32[1,1]{1,0:T(1,128)}, f32[16,2048]{1,0:T(8,128)}, f32[16,2048]{1,0:T(8,128)}, f32[2,16,2048]{2,1,0:T(8,128)}) custom-call(f32[1,1]{1,0:T(1,128)} %get-tuple-element.13.total_ref, f32[16,2048]{1,0:T(8,128)S(1)} %get-tuple-element.14.slope_ref, f32[2,16,2048]{2,1,0:T(8,128)S(1)} %get-tuple-element.15.fgrad_ref, ...), custom_call_target="tpu_custom_call" | custom-call | tf_op jit(solution)/shard_map/pallas_call | solution.py:702

commit v5 on v4

--- a/solution.py
+++ b/solution.py
@@ -87,8 +87,7 @@
     wyi = parts.reshape(256, 256)
     f128 = np.exp(-2j * np.pi * np.outer(s, s) / 128) * root
     ty = cplx(f128).T
-    tyi = cplx(f128.conj()).T
-    squares = np.stack([mx, my, wx, wxi, wy[:, :256], wy[:, 256:], wyi, ty, tyi])
+    squares = np.stack([mx, my, wx, wxi, wy[:, :256], wy[:, 256:], wyi, ty])
 
     own = np.zeros((128, 2, 128))
     mirror = np.zeros((128, 2, 128))
@@ -126,7 +125,7 @@
     )
 
 
-MX, MY, WX, WXI, WYA, WYB, WYI, TY, TYI = range(9)
+MX, MY, WX, WXI, WYA, WYB, WYI, TY = range(8)
 NAMES = ("squares", "td", "ti", "places", "places_t", "twx", "twy", "twr")
 
 
@@ -331,7 +330,7 @@
 
 def waves_back(values, t):
     cos, sin = t["twy"][0], t["twy"][1]
-    z = left(t["squares"][TYI], cat([cat([re, im], 0) for re, im in values], 1))
+    z = left(t["inverse"], cat([cat([re, im], 0) for re, im in values], 1))
     rows = []
     for v in range(len(values)):
         part = z[:, 128 * v : 128 * v + 128]
@@ -366,7 +365,7 @@
 
 ROWS = dict(t=2, ug=4, f=4, goal=2, w=2, m=2, n=2, fg=4, qv=4, nx=2)
 KEYS = tuple(ROWS)
-DIRECT = ("ug", "w", "m", "qv", "f")
+DIRECT = ("ug", "w", "m", "qv", "f", "fg", "nx")
 
 
 def hops(offset):
@@ -376,16 +375,16 @@
 FAR_FIRST = sorted(range(peers - 1, 0, -1), key=lambda offset: -hops(offset))
 
 
-RECEIVED = tuple(key for key in KEYS if key not in ("qv", "nx"))
+RECEIVED = tuple(key for key in KEYS if key != "nx")
 
 
 def kernel(*refs):
     fields_hbm = refs[:3]
     tables_hbm = refs[3 : 3 + len(NAMES)]
     refs = refs[3 + len(NAMES) :]
-    objective_ref, slope_ref, fgrad_ref = refs[:3]
-    recv = dict(zip(("qv", "nx"), refs[3:5]))
-    refs = refs[5:]
+    objective_ref, grad_ref, fgrad_ref = refs[:3]
+    recv = dict(nx=refs[3])
+    refs = refs[4:]
     u_ref, t_ref, f_ref = refs[:3]
     refs = refs[3:]
     tables = dict(zip(NAMES, refs[: len(NAMES)]))
@@ -394,8 +393,8 @@
     refs = refs[len(KEYS) :]
     recv.update(zip(RECEIVED, refs[: len(RECEIVED)]))
     refs = refs[len(RECEIVED) :]
-    part_ref, mid_ref, near_ref, far_ref, g1_ref, g2_ref, forced_ref, goal_ref = refs[:8]
-    table_sem, send_sem, recv_sem, own_sem = refs[8:]
+    part_ref, mid_ref, near_ref, far_ref, g1_ref, g2_ref, forced_ref, goal_ref, inverse_ref = refs[:9]
+    table_sem, send_sem, recv_sem, own_sem = refs[9:]
 
     me = lax.axis_index("px") * 8 + lax.axis_index("py")
     barrier = pltpu.get_barrier_semaphore()
@@ -479,16 +478,21 @@
         for g in range(2):
             put(key, row + g, cat(tiles[8 * g : 8 * g + 8], 0).T)
 
-    def get_tiles(key):
+    def get_tiles(key, row=0):
         out = []
         for g in range(2):
-            block = get(key, g).T
+            block = get(key, row + g).T
             out += [block[16 * i : 16 * i + 16] for i in range(8)]
         return out
 
     for load in loads:
         load.wait()
-    t = tables
+    forward = tables["squares"]
+    inverse_ref[...] = forward[TY]
+    for half in range(2):
+        inverse_ref[half, :128, 128:] = forward[TY, half, 128:, :128]
+        inverse_ref[half, 128:, :128] = forward[TY, half, :128, 128:]
+    t = dict(tables, inverse=inverse_ref)
     u_tiles = tiles_of(u_ref)
     put_field("ug", 0, u_tiles)
     put_field("ug", 2, rows_derivative(u_tiles, t))
@@ -625,8 +629,9 @@
     sums = jnp.sum(flat(far_ref)[...], axis=0, keepdims=True)
     objective_ref[...] = (0.5 / (n * n)) * jnp.sum(sums, axis=1, keepdims=True)
     arrive("qv")
-    for i, tile in enumerate(rows_derivative(get_tiles("qv"), t)):
-        slope_ref[:, 128 * i : 128 * i + 128] = tile
+    slope = rows_derivative(get_tiles("qv"), t)
+    for i, tile in enumerate(get_tiles("qv", 2)):
+        grad_ref[:, 128 * i : 128 * i + 128] = tile + slope[i]
     arrive("nx")
     for key in KEYS:
         whole(key).wait_send()
@@ -635,27 +640,24 @@
 
 
 def finish(
-    total_ref, slope_ref, fgrad_ref, v_ref, nx_ref,
-    objective_out, grad_out, next_out, fgrad_out, grad, nexts, sems,
+    total_ref, grad_ref, fgrad_ref, nx_ref,
+    objective_out, grad_out, next_out, fgrad_out, nexts, sems,
 ):
     objective_out[...] = total_ref[...]
     copies = [
         pltpu.make_async_copy(src, dst, sems.at[i])
         for i, (src, dst) in enumerate(
-            ((fgrad_ref, fgrad_out), (grad, grad_out), (nexts, next_out))
+            ((fgrad_ref, fgrad_out), (grad_ref, grad_out), (nexts, next_out))
         )
     ]
     copies[0].start()
-    for ref, out, i, rows, first in ((v_ref, grad, 1, 4, 2), (nx_ref, nexts, 2, 2, 0)):
-        for g in range(2):
-            block = ref.reshape(rows * peers, 128)[pl.ds(first + g, peers, rows), :].T
-            for k in range(8):
-                at = 128 * (8 * g + k)
-                tile = block[16 * k : 16 * k + 16]
-                if i == 1:
-                    tile = tile + slope_ref[:, at : at + 128]
-                out[:, at : at + 128] = tile
-        copies[i].start()
+    copies[1].start()
+    for g in range(2):
+        block = nx_ref.reshape(2 * peers, 128)[pl.ds(g, peers, 2), :].T
+        for k in range(8):
+            at = 128 * (8 * g + k)
+            nexts[:, at : at + 128] = block[16 * k : 16 * k + 16]
+    copies[2].start()
     for copy in copies:
         copy.wait()
 
@@ -672,12 +674,12 @@
     )
     field = jax.ShapeDtypeStruct((16, n), f32)
     both = jax.ShapeDtypeStruct((2, 16, n), f32)
-    landing = [jax.ShapeDtypeStruct((peers, ROWS[key], 128), f32) for key in ("qv", "nx")]
-    total, slope, forcing_rows, v, nx = pl.pallas_call(
+    landing = jax.ShapeDtypeStruct((peers, ROWS["nx"], 128), f32)
+    total, grad_rows, forcing_rows, nx = pl.pallas_call(
         kernel,
-        out_shape=(jax.ShapeDtypeStruct((1, 1), f32), field, both, *landing),
+        out_shape=(jax.ShapeDtypeStruct((1, 1), f32), field, both, landing),
         in_specs=[hbm] * len(operands),
-        out_specs=(vmem,) * 5,
+        out_specs=(vmem,) * 4,
         scratch_shapes=[pltpu.VMEM(x.shape, x.dtype) for x in operands]
         + [message(key) for key in KEYS]
         + [message(key) for key in RECEIVED]
@@ -690,6 +692,7 @@
             pltpu.VMEM((128, 256), f32),
             pltpu.VMEM((128, 256), f32),
             pltpu.VMEM((4, 128, 128), f32),
+            pltpu.VMEM((2, 256, 256), bf16),
             pltpu.SemaphoreType.DMA((len(operands),)),
             pltpu.SemaphoreType.DMA((len(KEYS) + 2,)),
             pltpu.SemaphoreType.DMA((len(KEYS) + 2,)),
@@ -702,15 +705,14 @@
     objective, field_grad, next_field, forcing_grad = pl.pallas_call(
         finish,
         out_shape=(jax.ShapeDtypeStruct((1, 1), f32), field, field, both),
-        in_specs=[vmem] * 5,
+        in_specs=[vmem] * 4,
         out_specs=(vmem,) + (hbm,) * 3,
         scratch_shapes=[
-            pltpu.VMEM((16, n), f32),
             pltpu.VMEM((16, n), f32),
             pltpu.SemaphoreType.DMA((3,)),
         ],
         compiler_params=pltpu.CompilerParams(vmem_limit_bytes=8 * 1024 * 1024),
-    )(total, slope, forcing_rows, v, nx)
+    )(total, grad_rows, forcing_rows, nx)
     return next_field[None], objective.reshape(()), field_grad[None], forcing_grad
 
 

time: 47.4 us -> 47.1 us (level)
  no operation moved by 1% of the time
where the time goes in v5:
time: 47.1 us; the launch traced here: 47 us
  Pallas kernels  46.3 us (98%)
  between operations  0.64 us (1%)
    pallas_call x1, Pallas kernels, per_device(): pl.pallas_call(kernel, out_shape=(jax.ShapeDtypeStruct((1, 1), f32), fiel...  44.4 us
    pallas_call x1, Pallas kernels, per_device(): pl.pallas_call(finish, out_shape=(jax.ShapeDtypeStruct((1, 1), f32), fiel...  1.96 us

profile of v5, /device:TPU:1, one launch (start us, length us, event | category | flops | bytes accessed | tf_op | source)
XLA Modules:
  0.0 47.0 jit_solution(12871223135879249243)
XLA Ops:
  0.6 44.4 %shard_map.138 = (f32[1,1]{1,0:T(1,128)}, f32[16,2048]{1,0:T(8,128)S(1)}, f32[2,16,2048]{2,1,0:T(8,128)S(1)}, f32[128,2,128]{2,1,0:T(2,128)S(1)}) custom-call(f32[16,2048]{1,0:T(8,128)} %bitcast.5, f32[16,2048]{1,0:T(8,128)} %bitcast.6, f32[2,16,2048]{2,1,0:T(8,128)} %refs_2_.1, bf16[8,2,256,256]{3,2,1,0:T(8,128)(2,1)} %constant.16.clone.refs_3_, ...), custom_call_target="tpu_custom_call" | custom-call | tf_op jit(solution)/shard_map/pallas_call | solution.py:678
  45.0 2.0 %shard_map.139 = (f32[1,1]{1,0:T(1,128)}, f32[16,2048]{1,0:T(8,128)}, f32[16,2048]{1,0:T(8,128)}, f32[2,16,2048]{2,1,0:T(8,128)}) custom-call(f32[1,1]{1,0:T(1,128)} %get-tuple-element.12.total_ref, f32[16,2048]{1,0:T(8,128)S(1)} %get-tuple-element.13.grad_ref, f32[2,16,2048]{2,1,0:T(8,128)S(1)} %get-tuple-element.14.fgrad_ref, ...), custom_call_target="tpu_custom_call" | custom-call | tf_op jit(solution)/shard_map/pallas_call | solution.py:705
